TPU v7x, 32 devices: a whole 2x2x4 slice. The times are simulated.
32 devices in a mesh: dp: 16 (over z, y, x), mp: 2 (over core).
Axes of the slice: x: 2, y: 2, z: 4, core: 2. Of those that a mesh axis runs over, the one named last changes fastest.
Arguments:
- block_input: bfloat16 [4096, 1792], P(('dp', 'mp')), may hold values from -45 to 45
- attn_gain: bfloat16 [1792], P('dp'), may hold values from 0.25 to 1.75
- query_weight: bfloat16 [1792, 1024], P('dp', 'mp')
- key_weight: bfloat16 [1792, 128], P('dp', 'mp')
- value_weight: bfloat16 [1792, 128], P('dp', 'mp'), may hold values from -0.125 to 0.125
- output_weight: bfloat16 [1024, 1792], P(('mp', 'dp')), may hold values from -1.5 to 1.5
- ffn_gain: bfloat16 [1792], P('dp'), may hold values from 0.25 to 1.75
- gate_weight: bfloat16 [1792, 2816], P('dp', 'mp'), may hold values from -0.125 to 0.125
- up_weight: bfloat16 [1792, 2816], P('dp', 'mp'), may hold values from -0.125 to 0.125
- down_weight: bfloat16 [2816, 1792], P(('mp', 'dp')), may hold values from -0.109375 to 0.109375
- output_cotangent: bfloat16 [4096, 1792], P(('dp', 'mp')), may hold values from -6 to 6
Outputs:
- block_output: bfloat16 [4096, 1792], P(('dp', 'mp'))
- input_grad: float32 [4096, 1792], P(('dp', 'mp'))
- attn_gain_grad: float32 [1792], P('dp')
- query_grad: float32 [1792, 1024], P('dp', 'mp')
- key_grad: float32 [1792, 128], P('dp', 'mp')
- value_grad: float32 [1792, 128], P('dp', 'mp')
- output_weight_grad: float32 [1024, 1792], P(('mp', 'dp'))
- ffn_gain_grad: float32 [1792], P('dp')
- gate_grad: float32 [1792, 2816], P('dp', 'mp')
- up_grad: float32 [1792, 2816], P('dp', 'mp')
- down_grad: float32 [2816, 1792], P(('mp', 'dp'))
All inputs are finite; a program needn't handle non-finite values.
Results may differ from a plain program's by a relative error of at most 0.012.
The roundings to bfloat16 on the way count: a program that leaves them out, or rounds other values in their place, can miss the bound.
Values may be sent and summed in bfloat16 or wider, within the bound.
A program may use at most 128 MiB of HBM per device.

v0:
```python
import functools

import jax
import jax.numpy as jnp
from jax import lax
from jax.experimental import pallas as pl
from jax.experimental.pallas import tpu as pltpu
from jax.sharding import PartitionSpec as P


HD = 64


EPSILON = 1e-05
ROPE_BASE = 10000.0


def rope_tables(length, head_dim):
    half_dim = head_dim // 2
    position = jnp.arange(length, dtype=jnp.float32)
    inverse = ROPE_BASE ** (-(jnp.arange(half_dim, dtype=jnp.float32) * (2.0 / head_dim)))
    angle = position[:, None] * inverse[None, :]
    return (jnp.cos(angle), jnp.sin(angle))


def rotate(values, cosine, sine):
    half_dim = values.shape[-1] // 2
    first_half = values[..., :half_dim]
    second_half = values[..., half_dim:]
    cos_part = cosine[:, None, :]
    sin_part = sine[:, None, :]
    return jnp.concatenate(
        [
            first_half * cos_part - second_half * sin_part,
            second_half * cos_part + first_half * sin_part,
        ],
        axis=-1,
    )


def unrotate(values, cosine, sine):
    half_dim = values.shape[-1] // 2
    first_half = values[..., :half_dim]
    second_half = values[..., half_dim:]
    cos_part = cosine[:, None, :]
    sin_part = sine[:, None, :]
    return jnp.concatenate(
        [
            first_half * cos_part + second_half * sin_part,
            second_half * cos_part - first_half * sin_part,
        ],
        axis=-1,
    )


def norm_scale(values):
    return lax.rsqrt(jnp.mean(values * values, axis=-1, keepdims=True) + EPSILON)


def norm_backward(values, inverse, gain, normed_cot):
    scaled = normed_cot * gain.astype(jnp.float32)[None, :]
    gain_grad = jnp.sum(normed_cot * values * inverse, axis=0)
    values_grad = inverse * scaled - values * (inverse * inverse * inverse) * jnp.mean(
        scaled * values, axis=-1, keepdims=True
    )
    return (gain_grad, values_grad)


def causal_scores(query_group, key_group):
    scale = query_group.shape[-1] ** (-0.5)
    scores = (
        jnp.einsum("qgd,kd->gqk", query_group, key_group, preferred_element_type=jnp.float32)
        * scale
    )
    length = key_group.shape[0]
    visible = lax.broadcasted_iota(jnp.int32, (length, length), 0) >= lax.broadcasted_iota(
        jnp.int32, (length, length), 1
    )
    return jnp.where(visible[None], scores, -jnp.inf)


def head_forward(parts):
    query_group, key_group, value_group = parts
    scores = causal_scores(query_group, key_group)
    top_score = jnp.max(scores, axis=-1, keepdims=True)
    log_norm = top_score + jnp.log(jnp.sum(jnp.exp(scores - top_score), axis=-1, keepdims=True))
    probs_b = jnp.exp(scores - log_norm).astype(jnp.bfloat16)
    attended = jnp.einsum(
        "gqk,kd->qgd", probs_b, value_group, preferred_element_type=jnp.float32
    ).astype(jnp.bfloat16)
    return (attended, log_norm[..., 0])


def head_backward(parts):
    query_group, key_group, value_group, attended, log_norm, attended_cot = parts
    scale = query_group.shape[-1] ** (-0.5)
    scores = causal_scores(query_group, key_group)
    probs = jnp.exp(scores - log_norm[..., None])
    probs_b = probs.astype(jnp.bfloat16)
    value_cot = jnp.einsum("gqk,qgd->kd", probs_b, attended_cot, preferred_element_type=jnp.float32)
    probs_cot = jnp.einsum(
        "qgd,kd->gqk", attended_cot, value_group, preferred_element_type=jnp.float32
    )
    delta = jnp.sum(attended_cot.astype(jnp.float32) * attended.astype(jnp.float32), axis=-1).T
    score_cot = (probs * (probs_cot - delta[:, :, None])).astype(jnp.bfloat16)
    query_cot = (
        jnp.einsum("gqk,kd->qgd", score_cot, key_group, preferred_element_type=jnp.float32) * scale
    )
    key_cot = (
        jnp.einsum("gqk,qgd->kd", score_cot, query_group, preferred_element_type=jnp.float32)
        * scale
    )
    return (query_cot, key_cot, value_cot)


def plain_shards(
    block_input,
    attn_gain,
    query_weight,
    key_weight,
    value_weight,
    output_weight,
    ffn_gain,
    gate_weight,
    up_weight,
    down_weight,
    output_cotangent,
):
    local_rows = block_input.shape[0]
    own_start = lax.axis_index("mp") * local_rows
    query_full, key_full, value_full, out_full, gain_one = (
        lax.all_gather(query_weight, "dp", axis=0, tiled=True),
        lax.all_gather(key_weight, "dp", axis=0, tiled=True),
        lax.all_gather(value_weight, "dp", axis=0, tiled=True),
        lax.all_gather(output_weight, "dp", axis=0, tiled=True),
        lax.all_gather(attn_gain, "dp", axis=0, tiled=True),
    )
    seq_input = lax.all_gather(block_input, "mp", axis=0, tiled=True)
    length = seq_input.shape[0]
    local_heads = query_full.shape[1] // HD
    local_groups = key_full.shape[1] // HD
    per_group = local_heads // local_groups
    cosine, sine = rope_tables(length, HD)
    input_f32 = seq_input.astype(jnp.float32)
    inv_one = norm_scale(input_f32)
    normed_one = (input_f32 * inv_one * gain_one.astype(jnp.float32)[None, :]).astype(jnp.bfloat16)
    query_raw = jnp.dot(normed_one, query_full, preferred_element_type=jnp.float32)
    key_raw = jnp.dot(normed_one, key_full, preferred_element_type=jnp.float32)
    value_raw = jnp.dot(normed_one, value_full, preferred_element_type=jnp.float32)
    query_rot = rotate(query_raw.reshape(length, local_heads, HD), cosine, sine).astype(
        jnp.bfloat16
    )
    key_rot = rotate(key_raw.reshape(length, local_groups, HD), cosine, sine).astype(jnp.bfloat16)
    value_b = value_raw.astype(jnp.bfloat16)
    query_groups = query_rot.reshape(length, local_groups, per_group, HD).transpose(1, 0, 2, 3)
    key_groups = key_rot.transpose(1, 0, 2)
    value_groups = value_b.reshape(length, local_groups, HD).transpose(1, 0, 2)
    attended, log_norm = lax.map(head_forward, (query_groups, key_groups, value_groups))
    attn_rows = attended.transpose(1, 0, 2, 3).reshape(length, local_heads * HD)
    attn_part = jnp.dot(attn_rows, out_full, preferred_element_type=jnp.float32)
    residual = input_f32 + lax.psum(attn_part, "mp")
    gate_full, up_full, down_full, gain_two = (
        lax.all_gather(gate_weight, "dp", axis=0, tiled=True),
        lax.all_gather(up_weight, "dp", axis=0, tiled=True),
        lax.all_gather(down_weight, "dp", axis=0, tiled=True),
        lax.all_gather(ffn_gain, "dp", axis=0, tiled=True),
    )
    inv_two = norm_scale(residual)
    normed_two = (residual * inv_two * gain_two.astype(jnp.float32)[None, :]).astype(jnp.bfloat16)
    gate_raw = jnp.dot(normed_two, gate_full, preferred_element_type=jnp.float32)
    up_raw = jnp.dot(normed_two, up_full, preferred_element_type=jnp.float32)
    sigma = jax.nn.sigmoid(gate_raw)
    hidden = (gate_raw * sigma * up_raw).astype(jnp.bfloat16)
    ffn_own = lax.psum_scatter(
        jnp.dot(hidden, down_full, preferred_element_type=jnp.float32),
        "mp",
        scatter_dimension=0,
        tiled=True,
    )
    residual_own = lax.dynamic_slice_in_dim(residual, own_start, local_rows, 0)
    block_output = (residual_own + ffn_own).astype(jnp.bfloat16)
    cot_seq = lax.all_gather(output_cotangent, "mp", axis=0, tiled=True)
    hidden_cot = jnp.einsum("td,fd->tf", cot_seq, down_full, preferred_element_type=jnp.float32)
    gate_cot = (hidden_cot * up_raw * sigma * (1.0 + gate_raw * (1.0 - sigma))).astype(jnp.bfloat16)
    up_cot = (hidden_cot * gate_raw * sigma).astype(jnp.bfloat16)
    normed_two_part = jnp.einsum(
        "tf,df->td", gate_cot, gate_full, preferred_element_type=jnp.float32
    )
    normed_two_part = normed_two_part + jnp.einsum(
        "tf,df->td", up_cot, up_full, preferred_element_type=jnp.float32
    )
    normed_two_cot = lax.psum(normed_two_part, "mp")
    ffn_gain_grad, residual_part = norm_backward(residual, inv_two, gain_two, normed_two_cot)
    residual_cot = cot_seq.astype(jnp.float32) + residual_part
    down_grad = jnp.einsum("tf,td->fd", hidden, cot_seq, preferred_element_type=jnp.float32)
    gate_grad = jnp.einsum("td,tf->df", normed_two, gate_cot, preferred_element_type=jnp.float32)
    up_grad = jnp.einsum("td,tf->df", normed_two, up_cot, preferred_element_type=jnp.float32)
    gate_share, up_share, down_share, ffn_gain_share = (
        lax.psum_scatter(gate_grad, "dp", scatter_dimension=0, tiled=True),
        lax.psum_scatter(up_grad, "dp", scatter_dimension=0, tiled=True),
        lax.psum_scatter(down_grad, "dp", scatter_dimension=0, tiled=True),
        lax.psum_scatter(ffn_gain_grad, "dp", scatter_dimension=0, tiled=True),
    )
    residual_cot_b = residual_cot.astype(jnp.bfloat16)
    output_weight_grad = jnp.einsum(
        "th,td->hd", attn_rows, residual_cot_b, preferred_element_type=jnp.float32
    )
    attended_cot = jnp.einsum(
        "td,hd->th", residual_cot_b, out_full, preferred_element_type=jnp.float32
    ).astype(jnp.bfloat16)
    cot_groups = attended_cot.reshape(length, local_groups, per_group, HD).transpose(1, 0, 2, 3)
    query_parts, key_parts, value_parts = lax.map(
        head_backward, (query_groups, key_groups, value_groups, attended, log_norm, cot_groups)
    )
    query_cot = (
        unrotate(query_parts.transpose(1, 0, 2, 3).reshape(length, local_heads, HD), cosine, sine)
        .reshape(length, local_heads * HD)
        .astype(jnp.bfloat16)
    )
    key_cot = (
        unrotate(key_parts.transpose(1, 0, 2), cosine, sine)
        .reshape(length, local_groups * HD)
        .astype(jnp.bfloat16)
    )
    value_cot = (
        value_parts.transpose(1, 0, 2).reshape(length, local_groups * HD).astype(jnp.bfloat16)
    )
    normed_one_part = jnp.einsum(
        "th,dh->td", query_cot, query_full, preferred_element_type=jnp.float32
    )
    normed_one_part = normed_one_part + jnp.einsum(
        "th,dh->td", key_cot, key_full, preferred_element_type=jnp.float32
    )
    normed_one_part = normed_one_part + jnp.einsum(
        "th,dh->td", value_cot, value_full, preferred_element_type=jnp.float32
    )
    normed_one_cot = lax.psum(normed_one_part, "mp")
    query_grad = jnp.einsum("td,th->dh", normed_one, query_cot, preferred_element_type=jnp.float32)
    key_grad = jnp.einsum("td,th->dh", normed_one, key_cot, preferred_element_type=jnp.float32)
    value_grad = jnp.einsum("td,th->dh", normed_one, value_cot, preferred_element_type=jnp.float32)
    attn_gain_grad, input_part = norm_backward(input_f32, inv_one, gain_one, normed_one_cot)
    input_cot = residual_cot + input_part
    input_grad = lax.dynamic_slice_in_dim(input_cot, own_start, local_rows, 0)
    attn_gain_share, query_share, key_share, value_share, output_share = (
        lax.psum_scatter(attn_gain_grad, "dp", scatter_dimension=0, tiled=True),
        lax.psum_scatter(query_grad, "dp", scatter_dimension=0, tiled=True),
        lax.psum_scatter(key_grad, "dp", scatter_dimension=0, tiled=True),
        lax.psum_scatter(value_grad, "dp", scatter_dimension=0, tiled=True),
        lax.psum_scatter(output_weight_grad, "dp", scatter_dimension=0, tiled=True),
    )
    return (
        block_output,
        input_grad,
        attn_gain_share,
        query_share,
        key_share,
        value_share,
        output_share,
        ffn_gain_share,
        gate_share,
        up_share,
        down_share,
    )


GROUP = 4
LANES = 128


def whole_up(size, step):
    return -(-size // step) * step


def partner(values, key):
    pairs = [(at, at ^ key) for at in range(lax.axis_size("dp"))]
    return lax.ppermute(values, "dp", pairs)


def across(values, key):
    pairs = [(at, at ^ (key * GROUP)) for at in range(lax.axis_size("dp"))]
    return lax.ppermute(values, "dp", pairs)


def after(value, *marks):
    return lax.optimization_barrier((value,) + marks)[0]


def narrowed(values, scale):
    return (values * scale).astype(jnp.float16)


def added(total, messages, undo):
    come = sum(message.astype(jnp.float32) for message in messages)
    return total + (come * undo).reshape(total.shape)


def messages_of(blocks, scale, at):
    return [
        narrowed(lax.dynamic_index_in_dim(blocks, at ^ key, 0, keepdims=False), scale)
        for key in range(1, blocks.shape[0])
    ]


def noted(values, scale, notes):
    return jnp.concatenate([values * scale, notes], axis=0).astype(jnp.float16)


def undo_of(message):
    return jnp.prod(message[-8:].astype(jnp.float32), axis=0, keepdims=True)


def group_messages(blocks, place, scale, notes):
    cols = blocks.shape[3]
    return [
        noted(
            lax.dynamic_index_in_dim(blocks, place ^ key, 1, keepdims=False).reshape(-1, cols),
            scale,
            notes,
        )
        for key in range(1, GROUP)
    ]


def line_messages(blocks, undo, at):
    power = jnp.log2(undo)
    row = lax.broadcasted_iota(jnp.float32, (8, undo.shape[1]), 0)
    notes = jnp.exp2(jnp.floor((jnp.round(power) + row) * 0.125))
    scale, notes = lax.optimization_barrier((1.0 / undo, notes))
    return [
        noted(lax.dynamic_index_in_dim(blocks, at ^ key, 0, keepdims=False), scale, notes)
        for key in range(1, blocks.shape[0])
    ]


def added_noted(total, messages, undos):
    for message, undo in zip(messages, undos):
        total = total + (message[:-8].astype(jnp.float32) * undo).reshape(total.shape)
    return total


def raised(undo, undos):
    for other in undos:
        undo = jnp.maximum(undo, other)
    return 4.0 * undo


def exchanged(messages, exchange):
    return [exchange(message, key + 1) for key, message in enumerate(messages)]


MESH = pl.DeviceIdType.MESH


def flipped(place, key):
    if key == 1:
        return place + 1 - 2 * lax.rem(place, 2)
    if key == 2:
        return place + 2 - 4 * lax.div(place, 2)
    return GROUP - 1 - place


class Wires:
    def __init__(self, send_sem):
        self.send_sem, self.used, self.open = send_sem, 0, []

    def send(self, source, target, arrival, device, when=None):
        copy = pltpu.make_async_remote_copy(
            src_ref=source,
            dst_ref=target,
            send_sem=self.send_sem.at[self.used],
            recv_sem=arrival,
            device_id=device,
            device_id_type=MESH,
        )
        self.used += 1
        self.open.append((copy, when))
        if when is None:
            copy.start()
        else:
            pl.when(when)(copy.start)

    def arrived(self, target, arrival, device, when=None):
        copy = pltpu.make_async_remote_copy(
            src_ref=target,
            dst_ref=target,
            send_sem=self.send_sem.at[0],
            recv_sem=arrival,
            device_id=device,
            device_id_type=MESH,
        )
        if when is None:
            copy.wait_recv()
        else:
            pl.when(when)(copy.wait_recv)

    def drain(self):
        for copy, when in self.open:
            if when is None:
                copy.wait_send()
            else:
                pl.when(when)(copy.wait_send)


class Seat:
    def __init__(self, lines):
        self.index = lax.axis_index("dp")
        self.core = lax.axis_index("mp")
        self.own, self.place = lax.div(self.index, GROUP), lax.rem(self.index, GROUP)
        self.lines = lines

    def mate(self, key):
        return (self.own * GROUP + flipped(self.place, key), self.core)

    def line(self, step):
        return ((self.own + step) * GROUP + self.place, self.core)

    def peer(self, key):
        return (flipped(self.own, key) * GROUP + self.place, self.core)

    def twin(self):
        return (self.index, 1 - self.core)

    def greet(self):
        barrier = pltpu.get_barrier_semaphore()
        for key in range(1, GROUP):
            pl.semaphore_signal(barrier, 1, device_id=self.mate(key), device_id_type=MESH)
        pl.semaphore_signal(barrier, 1, device_id=self.twin(), device_id_type=MESH)
        above, below = self.own < self.lines - 1, self.own > 0

        @pl.when(above)
        def _():
            pl.semaphore_signal(barrier, 1, device_id=self.line(1), device_id_type=MESH)

        @pl.when(below)
        def _():
            pl.semaphore_signal(barrier, 1, device_id=self.line(-1), device_id_type=MESH)

        ends = lax.div(self.own, self.lines - 1) + 1 - lax.div(self.own + self.lines - 1, self.lines)
        pl.semaphore_wait(barrier, GROUP + 2 - ends)


class Staged:
    def __init__(self, sems):
        self.sems, self.used, self.loads, self.stores = sems, 0, [], []

    def add(self, source, middle, target):
        load = pltpu.make_async_copy(source, middle, self.sems.at[self.used])
        store = pltpu.make_async_copy(middle, target, self.sems.at[self.used + 1])
        self.used += 2
        load.start()
        self.loads.append((load, store))

    def forward(self):
        for load, store in self.loads:
            load.wait()
            store.start()
            self.stores.append(store)
        self.loads = []

    def finish(self):
        for store in self.stores:
            store.wait()


def line_hop(wires, seat, arrays, hop):
    lines = seat.lines
    for blocks, arrivals in arrays:
        for step in (1, -1):
            from_block = seat.own - step * (hop - 1)
            into = seat.own + step
            ok = (from_block >= 0) & (from_block < lines) & (into >= 0) & (into < lines)
            block = blocks.at[lax.rem(from_block + lines, lines)]
            wires.send(
                block, block, arrivals.at[lax.rem(from_block + lines, lines)], seat.line(step), ok
            )


def line_landed(wires, seat, arrays, hop):
    lines = seat.lines
    for blocks, arrivals in arrays:
        for step in (1, -1):
            block = seat.own - step * hop
            ok = (block >= 0) & (block < lines)
            block = lax.rem(block + lines, lines)
            wires.arrived(blocks.at[block], arrivals.at[block], seat.twin(), ok)


def spread_own(wires, seat, own, rows, arrivals):
    for key in range(1, GROUP):
        wires.send(own, rows.at[0, key], arrivals.at[0, key], seat.mate(key))
    wires.send(own, rows.at[1, 0], arrivals.at[1, 0], seat.twin())


def spread_on(wires, seat, rows, arrivals):
    for key in range(1, GROUP):
        wires.arrived(rows.at[0, key], arrivals.at[0, key], seat.twin())
        wires.send(rows.at[0, key], rows.at[1, key], arrivals.at[1, key], seat.twin())


def spread_landed(wires, seat, rows, arrivals):
    for key in range(GROUP):
        wires.arrived(rows.at[1, key], arrivals.at[1, key], seat.twin())


def whole_gain(gains, which, rows):
    members = gains.shape[0]
    width = members * rows
    lane = lax.broadcasted_iota(jnp.int32, (1, LANES), 1)
    chunks = []
    for start in range(0, width, LANES):
        block = start // rows
        shift = block * rows - start
        chunk = gains[block, which : which + 1, :].astype(jnp.float32)
        chunk = pltpu.roll(chunk, shift % LANES, 1) if shift else chunk
        edge = rows + shift
        while edge < LANES and block + 1 < members:
            block += 1
            more = gains[block, which : which + 1, :].astype(jnp.float32)
            more = pltpu.roll(more, edge, 1) if edge % LANES else more
            chunk = jnp.where(lane < edge, chunk, more)
            edge += rows
        chunks.append(chunk)
    return jnp.concatenate(chunks, axis=1)


def turned(values, cosine, sine):
    half = HD // 2
    lane = lax.broadcasted_iota(jnp.int32, values.shape, 1)
    ahead = pltpu.roll(values, LANES - half, 1)
    behind = pltpu.roll(values, half, 1)
    other = jnp.where(lax.rem(lane, HD) < half, ahead, behind)
    return values * cosine + other * sine


def masked_scores(query, key):
    scores = lax.dot_general(
        query, key, (((1,), (1,)), ((), ())), preferred_element_type=jnp.float32
    ) * (HD**-0.5)
    row = lax.broadcasted_iota(jnp.int32, scores.shape, 0)
    column = lax.broadcasted_iota(jnp.int32, scores.shape, 1)
    return jnp.where(row >= column, scores, -jnp.inf)


def probabilities(query, key):
    scores = masked_scores(query, key)
    top = jnp.max(scores, axis=1, keepdims=True)
    log_norm = top + jnp.log(jnp.sum(jnp.exp(scores - top), axis=1, keepdims=True))
    return jnp.exp(scores - log_norm)


def norm_rows(source, start, count):
    values = source[pl.ds(start, count), :].astype(jnp.float32)
    inverse = lax.rsqrt(jnp.mean(values * values, axis=1, keepdims=True) + EPSILON)
    return values, inverse


STEP = 32


def attend_forward(normed, narrow, raw, heads, attended, tables):
    pairs = attended.shape[1] // LANES
    raw[...] = jnp.dot(normed[...], narrow[...], preferred_element_type=jnp.float32)
    last = pairs * LANES
    heads[:, last:] = turned(raw[:, last:], tables[2], tables[3]).astype(jnp.bfloat16)

    def pair(at, carry):
        lanes = pl.ds(pl.multiple_of(at * LANES, LANES), LANES)
        query = turned(raw[:, lanes], tables[0], tables[1]).astype(jnp.bfloat16)
        heads[:, lanes] = query
        key, value = heads[:, last : last + HD], heads[:, last + HD : last + 2 * HD]
        parts = []
        for head in range(LANES // HD):
            probs = probabilities(query[:, head * HD : (head + 1) * HD], key)
            parts.append(
                jnp.dot(probs.astype(jnp.bfloat16), value, preferred_element_type=jnp.float32)
            )
        attended[:, lanes] = jnp.concatenate(parts, axis=1).astype(jnp.bfloat16)
        return carry

    lax.fori_loop(0, pairs, pair, 0)


def front_kernel(
    lines,
    gains,
    narrow,
    out,
    pieces,
    down,
    inputs,
    cots,
    tables,
    gains_rows,
    narrow_full,
    out_full,
    wide,
    downs,
    cot_rows,
    rows,
    normed_one,
    heads_out,
    attended_out,
    residual_out,
    gains_v,
    narrow_v,
    out_v,
    piece_v,
    down_v,
    seq_v,
    cot_v,
    gain_v,
    tables_v,
    normed_v,
    raw_v,
    heads_v,
    attended_v,
    away_v,
    come_v,
    residual_v,
    second_v,
    stage_sem,
    load_sem,
    store_sem,
    send_sem,
    block_sem,
    mix_sem,
    line_sem,
    cot_sem,
    row_sem,
    seq_sem,
):
    seat = Seat(lines)
    wires, staged = Wires(send_sem), Staged(stage_sem)
    index, own, place, core = seat.index, seat.own, seat.place, seat.core
    count, half = narrow.shape[0], inputs.shape[0]
    out_count = out.shape[0]

    def slot(target, block):
        if target is gains_v:
            return gains_v.at[block]
        size = count if target is narrow_v else out_count
        return target.at[pl.ds(pl.multiple_of(block * size, 16), size)]

    def half_of(target, which):
        return target.at[pl.ds(pl.multiple_of(which * half, half), half)]

    loads = [
        pltpu.make_async_copy(source, target, load_sem.at[at])
        for at, (source, target) in enumerate(
            (
                (gains, slot(gains_v, index)),
                (narrow, slot(narrow_v, index)),
                (out, slot(out_v, index)),
                (inputs, half_of(seq_v, core)),
                (tables, tables_v),
            )
        )
    ]
    for load in loads:
        load.start()
    staged.add(pieces.at[place], piece_v, wide.at[own, place])
    staged.add(down, down_v, downs.at[own])
    staged.add(cots, cot_v, cot_rows.at[0, 0])
    seat.greet()
    whole = ((gains, gains_v, 0, 1, 2), (narrow, narrow_v, 1, 1, 2), (out, out_v, 2, 2, 1))

    def block_of(at, key=0):
        return lax.rem(at + lines, lines) * GROUP + (flipped(place, key) if key else place)

    def pass_on(target, which, block, device, ok=None):
        wires.send(slot(target, block), slot(target, block), block_sem.at[which, block], device, ok)

    def landed(target, which, block, ok=None):
        wires.arrived(slot(target, block), block_sem.at[which, block], seat.twin(), ok)

    for source, target, which, first, second in whole:
        for step in (1, -1):
            ok = (own + step >= 0) & (own + step < lines)
            wires.send(
                source, slot(target, index), block_sem.at[which, index], seat.line(step), ok
            )
        for key in (first, second):
            wires.send(source, slot(target, index), block_sem.at[which, index], seat.mate(key))
    for key in range(1, GROUP):
        wires.send(
            pieces.at[flipped(place, key)], wide.at[own, place], mix_sem.at[key], seat.mate(key)
        )
    wires.send(inputs, half_of(seq_v, core), seq_sem.at[0], seat.twin())
    staged.forward()
    for hop in range(1, lines):
        for _, target, which, first, second in whole:
            for step in (1, -1):
                at = own - step * hop
                ok = (at >= 0) & (at < lines)
                block = block_of(at)
                landed(target, which, block, ok)
                onward = ok & (own + step >= 0) & (own + step < lines)
                pass_on(target, which, block, seat.line(step), onward)
                for key in (first, second):
                    pass_on(target, which, block, seat.mate(key), ok)
        if hop == 1:
            for _, target, which, first, second in whole:
                block = block_of(own, first)
                landed(target, which, block)
                pass_on(target, which, block, seat.mate(second))
    staged.finish()
    for key in range(1, GROUP):
        wires.arrived(wide.at[own, flipped(place, key)], mix_sem.at[key], seat.twin())
    ffn = ((wide, line_sem.at[0]), (downs, line_sem.at[1]))
    line_hop(wires, seat, ffn, 1)
    for hop in range(1, lines):
        for _, target, which, first, second in whole:
            for step in (1, -1):
                at = own - step * hop
                ok = (at >= 0) & (at < lines)
                block = block_of(at, first)
                landed(target, which, block, ok)
                pass_on(target, which, block, seat.mate(second), ok)
    spread_own(wires, seat, cots, cot_rows, cot_sem)
    for load in loads:
        load.wait()
    wires.arrived(half_of(seq_v, 1 - core), seq_sem.at[0], seat.twin())
    for _, target, which, first, second in whole:
        for at in range(lines):
            for key in (second, GROUP - 1):
                landed(target, which, block_of(at, key))
    stores = []

    def put(source, target):
        store = pltpu.make_async_copy(source, target, store_sem.at[len(stores)])
        store.start()
        stores.append(store)

    put(narrow_v, narrow_full)
    put(out_v, out_full)
    for which in range(2):
        gain = whole_gain(gains_v, which, count)
        gain_v[pl.ds(which * 8, 8), :] = jnp.broadcast_to(gain, (8, gain.shape[1]))
    put(gain_v, gains_rows)

    def norm_one(at, carry):
        start = pl.multiple_of(at * STEP, STEP)
        values, inverse = norm_rows(seq_v, start, STEP)
        normed_v[pl.ds(start, STEP), :] = (values * inverse * gain_v[0:1, :]).astype(jnp.bfloat16)
        return carry

    lax.fori_loop(0, 2 * half // STEP, norm_one, 0)
    put(normed_v, normed_one)
    line_landed(wires, seat, ffn, 1)
    line_hop(wires, seat, ffn, 2)
    attend_forward(normed_v, narrow_v, raw_v, heads_v, attended_v, tables_v)
    put(heads_v, heads_out)
    put(attended_v, attended_out)

    def part_of(which):
        rows_of = attended_v[pl.ds(pl.multiple_of(which * half, half), half), :]
        return jnp.dot(rows_of, out_v[...], preferred_element_type=jnp.float32)

    away_v[...] = part_of(1 - core)
    wires.send(away_v, come_v, seq_sem.at[1], seat.twin())
    residual_v[...] = part_of(core)
    wires.arrived(come_v, seq_sem.at[1], seat.twin())

    def norm_two(at, carry):
        start = pl.multiple_of(at * STEP, STEP)
        span = pl.ds(start, STEP)
        values = seq_v[pl.ds(pl.multiple_of(core * half + start, STEP), STEP), :]
        residual_v[span, :] = values.astype(jnp.float32) + (residual_v[span, :] + come_v[span, :])
        values, inverse = norm_rows(residual_v, start, STEP)
        second_v[span, :] = (values * inverse * gain_v[8:9, :]).astype(jnp.bfloat16)
        return carry

    lax.fori_loop(0, half // STEP, norm_two, 0)
    spread_own(wires, seat, second_v, rows, row_sem)
    put(residual_v, residual_out)
    put(second_v, rows.at[0, 0])
    spread_on(wires, seat, cot_rows, cot_sem)
    line_landed(wires, seat, ffn, 2)
    for hop in range(3, lines):
        line_hop(wires, seat, ffn, hop)
    spread_on(wires, seat, rows, row_sem)
    spread_landed(wires, seat, cot_rows, cot_sem)
    spread_landed(wires, seat, rows, row_sem)
    for hop in range(3, lines):
        line_landed(wires, seat, ffn, hop)
    for store in stores:
        store.wait()
    wires.drain()


ANY = pl.BlockSpec(memory_space=pl.ANY)


def front(gains, narrow, out, pieces, down, inputs, cots, tables):
    members = lax.axis_size("dp")
    lines = members // GROUP
    bf16, f32 = gains.dtype, jnp.float32
    sources = (gains, narrow, out, pieces, down, inputs, cots, tables)
    _, cols = narrow.shape
    half, width = inputs.shape
    depth = members * out.shape[0]
    shape = jax.ShapeDtypeStruct
    results = [
        shape((16, width), f32),
        shape((width, cols), bf16),
        shape((depth, width), bf16),
        shape((lines,) + pieces.shape, bf16),
        shape((lines,) + down.shape, bf16),
        shape((2, GROUP, half, width), bf16),
        shape((2, GROUP, half, width), bf16),
        shape((2 * half, width), bf16),
        shape((2 * half, cols), bf16),
        shape((2 * half, depth), bf16),
        shape((half, width), f32),
    ]
    whole = 3
    sends = whole * (4 + (lines - 1) * 2 * 3 + 1 + (lines - 1) * 2) + 3 + 2 + 4 * (lines - 1) + 2 * 7
    dma = pltpu.SemaphoreType.DMA
    vmem = pltpu.VMEM
    return pl.pallas_call(
        functools.partial(front_kernel, lines),
        out_shape=results,
        in_specs=[ANY] * len(sources),
        out_specs=[ANY] * len(results),
        scratch_shapes=[
            vmem((members,) + gains.shape, bf16),
            vmem((width, cols), bf16),
            vmem((depth, width), bf16),
            vmem(pieces.shape[1:], bf16),
            vmem(down.shape, bf16),
            vmem((2 * half, width), bf16),
            vmem(cots.shape, bf16),
            vmem((16, width), f32),
            vmem(tables.shape, f32),
            vmem((2 * half, width), bf16),
            vmem((2 * half, cols), f32),
            vmem((2 * half, cols), bf16),
            vmem((2 * half, depth), bf16),
            vmem((half, width), f32),
            vmem((half, width), f32),
            vmem((half, width), f32),
            vmem((half, width), bf16),
            dma((6,)),
            dma((5,)),
            dma((8,)),
            dma((sends,)),
            dma((whole, members)),
            dma((GROUP,)),
            dma((2, lines)),
            dma((2, GROUP)),
            dma((2, GROUP)),
            dma((2,)),
        ],
        compiler_params=pltpu.CompilerParams(
            collective_id=0, has_side_effects=True, vmem_limit_bytes=40 << 20
        ),
        name="front",
    )(*sources)


SPAN = 14.0


def put_scales(tops, rows):
    power = jnp.clip(jnp.ceil(jnp.log2(jnp.maximum(tops, 1e-33))), -98.0, 126.0) - SPAN
    shape = rows.shape[1:]
    row = lax.broadcasted_iota(jnp.int32, shape, 0).astype(jnp.float32)
    rows[0] = jnp.broadcast_to(jnp.exp2(-power), shape)
    rows[1] = jnp.broadcast_to(jnp.exp2(power), shape)
    rows[2] = jnp.exp2(jnp.floor((power + row) * 0.125))


def tops_of(values):
    return jnp.max(jnp.abs(values), axis=0, keepdims=True)


def meet(seat):
    barrier = pltpu.get_barrier_semaphore()
    others = [seat.mate(key) for key in range(1, GROUP)]
    others += [seat.peer(key) for key in range(1, seat.lines)] + [seat.twin()]
    for other in others:
        pl.semaphore_signal(barrier, 1, device_id=other, device_id_type=MESH)
    pl.semaphore_wait(barrier, len(others))


def meet_twin(seat):
    barrier = pltpu.get_barrier_semaphore()
    pl.semaphore_signal(barrier, 1, device_id=seat.twin(), device_id_type=MESH)
    pl.semaphore_wait(barrier, 1)


def send_bounds(wires, mine, come, sems, devices, first):
    for at, device in enumerate(devices):
        wires.send(mine, come.at[first + at], sems.at[first + at], device)


def take_bounds(wires, seat, mine, come, sems, devices, first):
    bounds = mine[...]
    for at in range(len(devices)):
        wires.arrived(come.at[first + at], sems.at[first + at], seat.twin())
        bounds = jnp.maximum(bounds, come[first + at])
    return bounds


class Moves:
    def __init__(self, sems):
        self.sems, self.used, self.open = sems, 0, []

    def start(self, source, target):
        copy = pltpu.make_async_copy(source, target, self.sems.at[self.used])
        copy.start()
        self.used += 1
        return copy

    def put(self, source, target):
        self.open.append(self.start(source, target))

    def finish(self):
        for copy in self.open:
            copy.wait()


def dot_rows(left, right):
    return jnp.dot(left, right, preferred_element_type=jnp.float32)


def dot_across(left, right):
    return lax.dot_general(left, right, (((1,), (1,)), ((), ())), preferred_element_type=jnp.float32)


def dot_down(left, right):
    return lax.dot_general(left, right, (((0,), (0,)), ((), ())), preferred_element_type=jnp.float32)


CHUNK = 256


def sum_up(near, come):
    def step(at, carry):
        span = pl.ds(pl.multiple_of(at * STEP, STEP), STEP)
        near[span, :] = near[span, :] + come[span, :]
        return carry

    lax.fori_loop(0, near.shape[0] // STEP, step, 0)


def units_kernel(
    lines,
    share,
    rows,
    cots,
    wide,
    down,
    gains,
    hidden_out,
    back_out,
    wide_out,
    factors,
    wide_factors,
    rows_v,
    cots_v,
    wide_v,
    down_v,
    gains_v,
    hidden_v,
    both_v,
    far_v,
    near_v,
    come_v,
    wide_grad_v,
    mine_v,
    bounds_v,
    factors_v,
    wide_factors_v,
    move_sem,
    send_sem,
    come_sem,
    bound_sem,
):
    seat = Seat(lines)
    moves = Moves(move_sem)
    count, width = rows.shape
    half = count // 2
    padded = hidden_v.shape[1]
    chunks = half // CHUNK
    loads = []
    for source, target in ((wide, wide_v), (down, down_v.at[pl.ds(0, share)]), (gains, gains_v)):
        loads.append(moves.start(source, target))
    for at in range(2 * chunks):
        span = pl.ds((at * CHUNK + half) % count, CHUNK)
        loads.append(moves.start(rows.at[span], rows_v.at[span]))
        loads.append(moves.start(cots.at[span], cots_v.at[span]))
    down_v[share:, :] = jnp.zeros((padded - share, width), down_v.dtype)
    meet(seat)
    for load in loads[:3]:
        load.wait()
    wires = Wires(send_sem)
    back_top = jnp.zeros((1, width), jnp.float32)
    cot_top = jnp.zeros((1, width), jnp.bfloat16)
    hidden_sum = jnp.zeros((1, padded), jnp.float32)
    hidden_top = jnp.zeros((1, 1), jnp.float32)
    both_sum = jnp.zeros((1, 2 * padded), jnp.float32)
    for at in range(2 * chunks):
        loads[3 + 2 * at].wait()
        loads[4 + 2 * at].wait()
        start = (at * CHUNK + half) % count
        span = pl.ds(start, CHUNK)
        raw = dot_rows(rows_v[span, :], wide_v[...])
        hidden_cot = dot_across(cots_v[span, :], down_v[...])
        gate, up = raw[:, :padded], raw[:, padded:]
        sigma = jax.nn.sigmoid(gate)
        hidden = (gate * sigma * up).astype(jnp.bfloat16)
        hidden_v[span, :] = hidden
        both_v[span, :padded] = (
            hidden_cot * up * sigma * (1.0 + gate * (1.0 - sigma))
        ).astype(jnp.bfloat16)
        both_v[span, padded:] = (hidden_cot * gate * sigma).astype(jnp.bfloat16)
        part = dot_across(both_v[span, :], wide_v[...])
        back_top = jnp.maximum(back_top, tops_of(part))
        if start >= half:
            piece = pl.ds(start - half, CHUNK)
            far_v[piece, :] = part
            wires.send(far_v.at[piece], come_v.at[piece], come_sem.at[at], seat.twin())
        else:
            near_v[span, :] = part
        hidden_size = jnp.abs(hidden.astype(jnp.float32))
        hidden_sum += jnp.sum(hidden_size, axis=0, keepdims=True)
        across = jnp.sum(hidden_size, axis=1, keepdims=True)
        hidden_top = jnp.maximum(hidden_top, jnp.max(across, axis=0, keepdims=True))
        both_sum += jnp.sum(jnp.abs(both_v[span, :].astype(jnp.float32)), axis=0, keepdims=True)
        cot_top = jnp.maximum(cot_top, jnp.max(jnp.abs(cots_v[span, :]), axis=0, keepdims=True))
    gain_top = jnp.max(jnp.abs(gains_v[8:9, :]), axis=1, keepdims=True)
    down_top = jnp.max(jnp.abs(down_v[...]), axis=0, keepdims=True).astype(jnp.float32)
    mine_v[0:1, :] = 2.0 * back_top
    mine_v[1:2, :] = (
        1.1 * jnp.max(hidden_sum, axis=1, keepdims=True) * cot_top.astype(jnp.float32)
    )
    mine_v[2:3, :] = 2.2 * hidden_top * down_top
    mine_v[3:4, :] = jnp.zeros((1, width), jnp.float32)
    mine_v[3:4, : 2 * padded] = (1.1 * width**0.5) * gain_top * both_sum
    mine_v[4:8, :] = jnp.zeros((4, width), jnp.float32)
    mates = [seat.mate(key) for key in range(1, GROUP)]
    others = [seat.peer(key) for key in range(1, lines)] + [seat.twin()]
    send_bounds(wires, mine_v.at[pl.ds(0, 8)], bounds_v, bound_sem, mates, 0)
    moves.put(hidden_v, hidden_out)

    def wide_step(at, carry):
        span = pl.ds(pl.multiple_of(at * CHUNK, CHUNK), CHUNK)
        wide_grad_v[span, :] = dot_down(rows_v[:, span], both_v[...])
        return carry

    lax.fori_loop(0, width // CHUNK // 2, wide_step, 0)
    mine_v[8:, :] = take_bounds(
        wires, seat, mine_v.at[pl.ds(0, 8)], bounds_v, bound_sem, mates, 0
    )
    send_bounds(wires, mine_v.at[pl.ds(8, 8)], bounds_v, bound_sem, others, len(mates))
    lax.fori_loop(width // CHUNK // 2, width // CHUNK, wide_step, 0)
    moves.put(wide_grad_v, wide_out)
    for at in range(chunks):
        wires.arrived(come_v.at[pl.ds(at * CHUNK, CHUNK)], come_sem.at[at], seat.twin())
    sum_up(near_v, come_v)
    moves.put(near_v, back_out)
    bounds = take_bounds(
        wires, seat, mine_v.at[pl.ds(8, 8)], bounds_v, bound_sem, others[:-1], len(mates)
    )
    last = len(mates) + len(others) - 1
    wires.arrived(bounds_v.at[last], bound_sem.at[last], seat.twin())
    for at in range(3):
        bound = bounds[at : at + 1]
        if at != 1:
            bound = jnp.maximum(bound, bounds_v[last, at : at + 1, :])
        put_scales(bound, factors_v.at[at])
    put_scales(bounds[3:4, : 2 * padded], wide_factors_v)
    moves.put(factors_v, factors)
    moves.put(wide_factors_v, wide_factors)
    moves.finish()
    wires.drain()


HBM = pl.BlockSpec(memory_space=pltpu.HBM)


def units(rows, cots, wide, down, gains, padded):
    count, width = rows.shape
    half = count // 2
    share = down.shape[0]
    lines = lax.axis_size("dp") // GROUP
    f32, bf16 = jnp.float32, rows.dtype
    shape, vmem, dma = jax.ShapeDtypeStruct, pltpu.VMEM, pltpu.SemaphoreType.DMA
    chunks = half // CHUNK
    rounds = GROUP - 1 + lines
    return pl.pallas_call(
        functools.partial(units_kernel, lines, share),
        out_shape=[
            shape((count, padded), bf16),
            shape((half, width), f32),
            shape((width, 2 * padded), f32),
            shape((3, 3, 8, width), f32),
            shape((3, 8, 2 * padded), f32),
        ],
        in_specs=[HBM] * 5,
        out_specs=[HBM] * 5,
        scratch_shapes=[
            vmem((count, width), bf16),
            vmem((count, width), bf16),
            vmem(wide.shape, bf16),
            vmem((padded, width), bf16),
            vmem(gains.shape, f32),
            vmem((count, padded), bf16),
            vmem((count, 2 * padded), bf16),
            vmem((half, width), f32),
            vmem((half, width), f32),
            vmem((half, width), f32),
            vmem((width, 2 * padded), f32),
            vmem((16, width), f32),
            vmem((rounds, 8, width), f32),
            vmem((3, 3, 8, width), f32),
            vmem((3, 8, 2 * padded), f32),
            dma((3 + 4 * chunks + 5,)),
            dma((chunks + rounds,)),
            dma((chunks,)),
            dma((rounds,)),
        ],
        compiler_params=pltpu.CompilerParams(
            collective_id=1, has_side_effects=True, vmem_limit_bytes=48 << 20
        ),
        cost_estimate=pl.CostEstimate(flops=10**10, bytes_accessed=2 * 10**7, transcendentals=0),
        name="units",
    )(rows, cots, wide, down, gains)


def grads_kernel(
    lines,
    share,
    cots,
    hidden,
    down,
    down_out,
    forth_out,
    cots_v,
    hidden_v,
    down_v,
    down_grad_v,
    far_v,
    near_v,
    come_v,
    move_sem,
    send_sem,
    come_sem,
):
    seat = Seat(lines)
    moves = Moves(move_sem)
    count, width = cots.shape
    half = count // 2
    padded = hidden_v.shape[1]
    pairs = ((hidden, hidden_v), (down, down_v.at[pl.ds(0, share)]), (cots, cots_v))
    loads = [moves.start(source, target) for source, target in pairs]
    down_v[share:, :] = jnp.zeros((padded - share, width), down_v.dtype)
    meet_twin(seat)
    wires = Wires(send_sem)
    for load in loads[:2]:
        load.wait()
    far_v[...] = dot_rows(hidden_v[half:, :], down_v[...])
    wires.send(far_v, come_v, come_sem.at[0], seat.twin())
    loads[2].wait()

    def down_step(at, carry):
        span = pl.ds(pl.multiple_of(at * LANES, LANES), LANES)
        down_grad_v[span, :] = dot_down(hidden_v[:, span], cots_v[...])
        return carry

    lax.fori_loop(0, padded // LANES, down_step, 0)
    moves.put(down_grad_v.at[pl.ds(0, share)], down_out)
    near_v[...] = dot_rows(hidden_v[:half, :], down_v[...])
    wires.arrived(come_v, come_sem.at[0], seat.twin())
    sum_up(near_v, come_v)
    moves.put(near_v, forth_out)
    moves.finish()
    wires.drain()


def grads(cots, hidden, down):
    count, width = cots.shape
    half = count // 2
    padded = hidden.shape[1]
    share = down.shape[0]
    lines = lax.axis_size("dp") // GROUP
    f32, bf16 = jnp.float32, cots.dtype
    shape, vmem, dma = jax.ShapeDtypeStruct, pltpu.VMEM, pltpu.SemaphoreType.DMA
    return pl.pallas_call(
        functools.partial(grads_kernel, lines, share),
        out_shape=[shape((share, width), f32), shape((half, width), f32)],
        in_specs=[HBM] * 3,
        out_specs=[HBM] * 2,
        scratch_shapes=[
            vmem((count, width), bf16),
            vmem((count, padded), bf16),
            vmem((padded, width), bf16),
            vmem((padded, width), f32),
            vmem((half, width), f32),
            vmem((half, width), f32),
            vmem((half, width), f32),
            dma((3 + 2,)),
            dma((1,)),
            dma((1,)),
        ],
        compiler_params=pltpu.CompilerParams(
            collective_id=2, has_side_effects=True, vmem_limit_bytes=40 << 20
        ),
        cost_estimate=pl.CostEstimate(flops=10**10, bytes_accessed=2 * 10**7, transcendentals=0),
        name="grads",
    )(cots, hidden, down)


def split_gain(flat, block, rows):
    start = block * rows
    chunk, offset = start // LANES, start % LANES
    lane = lax.broadcasted_iota(jnp.int32, (1, LANES), 1)
    piece = flat[:, chunk * LANES : (chunk + 1) * LANES]
    piece = pltpu.roll(piece, LANES - offset, 1) if offset else piece
    if offset + rows > LANES:
        more = flat[:, (chunk + 1) * LANES : (chunk + 2) * LANES]
        piece = jnp.where(lane < LANES - offset, piece, pltpu.roll(more, LANES - offset, 1))
    return jnp.where(lane < rows, piece, 0.0)


def norm_back(values, inverse, gain, cot):
    scaled = cot * gain
    share = jnp.mean(scaled * values, axis=1, keepdims=True)
    return inverse * scaled - values * (inverse * inverse * inverse) * share


def folded(values):
    return jnp.sum(values.reshape(-1, 8, values.shape[1]), axis=0)


def step_rows(start, which, half):
    return pl.ds(pl.multiple_of(which * half + start, STEP), STEP)


def half_of(target, which):
    half = target.shape[0] // 2
    return target.at[pl.ds(pl.multiple_of(which * half, half), half)]


def turn_kernel(
    lines,
    second_cot,
    residual,
    gains,
    cots,
    attended,
    out_full,
    residual_cot,
    mix_out,
    out_grad,
    sums_out,
    out_factors,
    second_v,
    residual_v,
    gains_v,
    cots_v,
    attended_v,
    out_v,
    seq_v,
    mix_v,
    out_grad_v,
    sums_v,
    out_rows,
    move_sem,
    send_sem,
    come_sem,
):
    seat = Seat(lines)
    core = seat.core
    moves = Moves(move_sem)
    half, width = residual.shape
    depth = attended.shape[1]
    bf16 = attended_v.dtype
    pairs = (
        (second_cot, second_v),
        (residual, residual_v),
        (gains, gains_v),
        (cots, cots_v),
        (attended, attended_v),
        (out_full, out_v),
    )
    loads = [moves.start(source, target) for source, target in pairs]
    meet_twin(seat)
    wires = Wires(send_sem)
    for load in loads[:4]:
        load.wait()
    sums_v[...] = jnp.zeros_like(sums_v)

    def norm_two(at, carry):
        start = pl.multiple_of(at * STEP, STEP)
        span = pl.ds(start, STEP)
        values, inverse = norm_rows(residual_v, start, STEP)
        cot = second_v[span, :]
        sums_v[...] += folded(cot * values * inverse)
        total = cots_v[span, :].astype(jnp.float32) + norm_back(
            values, inverse, gains_v[8:9, :], cot
        )
        residual_v[span, :] = total
        seq_v[step_rows(start, core, half), :] = total.astype(bf16)
        return carry

    lax.fori_loop(0, half // STEP, norm_two, 0)
    wires.send(half_of(seq_v, core), half_of(seq_v, core), come_sem.at[0], seat.twin())
    moves.put(residual_v, residual_cot)
    moves.put(sums_v, sums_out)
    for load in loads[4:]:
        load.wait()
    wires.arrived(half_of(seq_v, 1 - core), come_sem.at[0], seat.twin())

    def out_step(at, top):
        span = pl.ds(pl.multiple_of(at * LANES, LANES), LANES)
        part = dot_down(attended_v[:, span], seq_v[...])
        out_grad_v[span, :] = part
        return jnp.maximum(top, tops_of(part))

    top = lax.fori_loop(0, depth // LANES, out_step, jnp.zeros((1, width), jnp.float32))
    moves.put(out_grad_v, out_grad)
    put_scales(top, out_rows)
    moves.put(out_rows, out_factors)
    mix_v[...] = dot_across(seq_v[...], out_v[...]).astype(bf16)
    moves.put(mix_v, mix_out)
    moves.finish()
    wires.drain()


def turn(second_cot, residual, gains, cots, attended, out_full):
    lines = lax.axis_size("dp") // GROUP
    half, width = residual.shape
    depth = attended.shape[1]
    f32, bf16 = jnp.float32, attended.dtype
    shape, vmem, dma = jax.ShapeDtypeStruct, pltpu.VMEM, pltpu.SemaphoreType.DMA
    sources = (second_cot, residual, gains, cots, attended, out_full)
    return pl.pallas_call(
        functools.partial(turn_kernel, lines),
        out_shape=[
            shape((half, width), f32),
            shape((2 * half, depth), bf16),
            shape((depth, width), f32),
            shape((8, width), f32),
            shape((3, 8, width), f32),
        ],
        in_specs=[HBM] * len(sources),
        out_specs=[HBM] * 5,
        scratch_shapes=[vmem(part.shape, part.dtype) for part in sources]
        + [
            vmem((2 * half, width), bf16),
            vmem((2 * half, depth), bf16),
            vmem((depth, width), f32),
            vmem((8, width), f32),
            vmem((3, 8, width), f32),
            dma((len(sources) + 5,)),
            dma((1,)),
            dma((1,)),
        ],
        compiler_params=pltpu.CompilerParams(
            collective_id=3, has_side_effects=True, vmem_limit_bytes=24 << 20
        ),
        cost_estimate=pl.CostEstimate(flops=10**10, bytes_accessed=2 * 10**7, transcendentals=0),
        name="turn",
    )(*sources)


def rear_kernel(
    lines,
    members,
    residual_cot,
    mix,
    sums,
    gains,
    inputs,
    heads,
    attended,
    narrow_full,
    normed,
    tables,
    input_grad,
    narrow_grad,
    narrow_factors,
    residual_v,
    mix_v,
    sums_in_v,
    gains_v,
    inputs_v,
    heads_v,
    attended_v,
    narrow_v,
    normed_v,
    tables_v,
    cot_v,
    pair_v,
    far_v,
    near_v,
    come_v,
    narrow_grad_v,
    sums_v,
    sums_come_v,
    gain_grad_v,
    narrow_rows,
    move_sem,
    send_sem,
    come_sem,
):
    seat = Seat(lines)
    core = seat.core
    moves = Moves(move_sem)
    half, width = inputs.shape
    depth = attended.shape[1]
    cols = heads.shape[1]
    count = width // members
    bf16 = heads_v.dtype
    pairs = (
        (mix, mix_v),
        (heads, heads_v),
        (attended, attended_v),
        (tables, tables_v),
        (narrow_full, narrow_v),
        (normed, normed_v),
        (residual_cot, residual_v),
        (sums, sums_in_v),
        (gains, gains_v),
        (inputs, inputs_v),
    )
    loads = [moves.start(source, target) for source, target in pairs]
    meet_twin(seat)
    wires = Wires(send_sem)
    for load in loads[:4]:
        load.wait()
    pair_v[...] = jnp.zeros_like(pair_v)

    def pair(at, carry):
        lanes = pl.ds(pl.multiple_of(at * LANES, LANES), LANES)
        key, value = heads_v[:, depth : depth + HD], heads_v[:, depth + HD : depth + 2 * HD]
        query_both, mix_both = heads_v[:, lanes], mix_v[:, lanes]
        delta_both = mix_both.astype(jnp.float32) * attended_v[:, lanes].astype(jnp.float32)
        parts = []
        for head in range(LANES // HD):
            own = slice(head * HD, (head + 1) * HD)
            query, mix_own = query_both[:, own], mix_both[:, own]
            probs = probabilities(query, key)
            value_part = dot_down(probs.astype(bf16), mix_own)
            delta = jnp.sum(delta_both[:, own], axis=1, keepdims=True)
            score_cot = (probs * (dot_across(mix_own, value) - delta)).astype(bf16)
            parts.append(dot_rows(score_cot, key) * (HD**-0.5))
            key_part = dot_down(score_cot, query) * (HD**-0.5)
            pair_v[...] += jnp.concatenate([key_part, value_part], axis=1)
        query_cot = turned(jnp.concatenate(parts, axis=1), tables_v[0], -tables_v[1])
        cot_v[:, lanes] = query_cot.astype(bf16)
        return carry

    lax.fori_loop(0, depth // LANES, pair, 0)
    cot_v[:, depth:] = turned(pair_v[...], tables_v[2], -tables_v[3]).astype(bf16)
    for load in loads[4:]:
        load.wait()

    def part_of(which):
        rows_of = cot_v[pl.ds(pl.multiple_of(which * half, half), half), :]
        return dot_across(rows_of, narrow_v[...])

    far_v[...] = part_of(1 - core)
    wires.send(far_v, come_v, come_sem.at[0], seat.twin())
    near_v[...] = part_of(core)

    def narrow_step(at, top):
        span = pl.ds(pl.multiple_of(at * CHUNK, CHUNK), CHUNK)
        part = dot_down(normed_v[:, span], cot_v[...])
        narrow_grad_v[span, :] = part
        return jnp.maximum(top, tops_of(part))

    top = lax.fori_loop(0, width // CHUNK, narrow_step, jnp.zeros((1, cols), jnp.float32))
    for block in range(members):
        moves.put(
            narrow_grad_v.at[pl.ds(block * count, count)], narrow_grad.at[block, pl.ds(0, count)]
        )
    wires.arrived(come_v, come_sem.at[0], seat.twin())
    sums_v[8:, :] = sums_in_v[...]
    sums_v[:8, :] = jnp.zeros_like(sums_in_v)

    def norm_one(at, carry):
        start = pl.multiple_of(at * STEP, STEP)
        span = pl.ds(start, STEP)
        values, inverse = norm_rows(inputs_v, start, STEP)
        cot = near_v[span, :] + come_v[span, :]
        sums_v[:8, :] += folded(cot * values * inverse)
        near_v[span, :] = residual_v[span, :] + norm_back(values, inverse, gains_v[0:1, :], cot)
        return carry

    lax.fori_loop(0, half // STEP, norm_one, 0)
    wires.send(sums_v, sums_come_v, come_sem.at[1], seat.twin())
    moves.put(near_v, input_grad)
    wires.arrived(sums_come_v, come_sem.at[1], seat.twin())
    both = sums_v[...] + sums_come_v[...]
    flat = [jnp.sum(both[8 * at : 8 * at + 8, :], axis=0, keepdims=True) for at in range(2)]
    gain_grad_v[...] = jnp.zeros_like(gain_grad_v)
    for block in range(members):
        for at in range(2):
            piece = split_gain(flat[at], block, count)
            gain_grad_v[block, 0:1, at * LANES : (at + 1) * LANES] = piece
            lanes = slice(at * LANES, (at + 1) * LANES)
            raised = jnp.maximum(top[:, lanes], jnp.abs(piece))
            top = jnp.concatenate(
                [part for part in (top[:, : at * LANES], raised, top[:, (at + 1) * LANES :]) if part.size],
                axis=1,
            )
    moves.put(gain_grad_v, narrow_grad.at[:, pl.ds(count, 8), :])
    put_scales(top, narrow_rows)
    moves.put(narrow_rows, narrow_factors)
    moves.finish()
    wires.drain()


def rear(residual_cot, mix, sums, gains, inputs, heads, attended, narrow_full, normed, tables):
    members = lax.axis_size("dp")
    lines = members // GROUP
    half, width = inputs.shape
    cols = heads.shape[1]
    count = width // members
    f32, bf16 = jnp.float32, heads.dtype
    shape, vmem, dma = jax.ShapeDtypeStruct, pltpu.VMEM, pltpu.SemaphoreType.DMA
    sources = (
        residual_cot,
        mix,
        sums,
        gains,
        inputs,
        heads,
        attended,
        narrow_full,
        normed,
        tables,
    )
    return pl.pallas_call(
        functools.partial(rear_kernel, lines, members),
        out_shape=[
            shape((half, width), f32),
            shape((members, count + 8, cols), f32),
            shape((3, 8, cols), f32),
        ],
        in_specs=[HBM] * len(sources),
        out_specs=[HBM] * 3,
        scratch_shapes=[vmem(part.shape, part.dtype) for part in sources]
        + [
            vmem((2 * half, cols), bf16),
            vmem((2 * half, LANES), f32),
            vmem((half, width), f32),
            vmem((half, width), f32),
            vmem((half, width), f32),
            vmem((width, cols), f32),
            vmem((16, width), f32),
            vmem((16, width), f32),
            vmem((members, 8, cols), f32),
            vmem((3, 8, cols), f32),
            dma((len(sources) + members + 3,)),
            dma((2,)),
            dma((2,)),
        ],
        compiler_params=pltpu.CompilerParams(
            collective_id=4, has_side_effects=True, vmem_limit_bytes=32 << 20
        ),
        cost_estimate=pl.CostEstimate(flops=10**10, bytes_accessed=2 * 10**7, transcendentals=0),
        name="rear",
    )(*sources)


def unshare_kernel(share, lines, pieces, gate, up):
    place = lax.rem(lax.axis_index("dp"), GROUP)
    unit_rows = share // lines
    padded = pieces.shape[2] // 2
    for start, target in ((0, gate), (padded, up)):
        parts = []
        for at in range(lines):
            for other in range(GROUP):
                piece = pieces[flipped(place, other) if other else place]
                first = start + at * unit_rows
                parts.append(piece[:, first : first + unit_rows])
        target[...] = jnp.concatenate(parts, axis=1)


def unshare(pieces, share, lines):
    rows = pieces.shape[1]
    result = jax.ShapeDtypeStruct((rows, GROUP * share), pieces.dtype)
    return pl.pallas_call(
        functools.partial(unshare_kernel, share, lines), out_shape=[result] * 2, name="unshare"
    )(pieces)


def grouped_shards(
    block_input,
    attn_gain,
    query_weight,
    key_weight,
    value_weight,
    output_weight,
    ffn_gain,
    gate_weight,
    up_weight,
    down_weight,
    output_cotangent,
):
    f32, bf16 = jnp.float32, jnp.bfloat16
    members = lax.axis_size("dp")
    lines = members // GROUP
    index = lax.axis_index("dp")
    own, place = index // GROUP, lax.rem(index, GROUP)
    rows, _ = gate_weight.shape
    width = rows * members
    query_cols, key_cols = query_weight.shape[1], key_weight.shape[1]
    unit_rows = down_weight.shape[0]
    share = unit_rows * lines
    padded = whole_up(share, LANES)

    narrow = jnp.concatenate([query_weight, key_weight, value_weight], axis=1)
    cols = narrow.shape[1]
    gains = jnp.stack([attn_gain, ffn_gain])
    gains = jnp.pad(gains, ((0, 6), (0, whole_up(rows, LANES) - rows)))

    def shares(weight):
        parts = weight.reshape(rows, lines, GROUP, unit_rows).transpose(2, 0, 1, 3)
        return jnp.pad(parts.reshape(GROUP, rows, share), ((0, 0), (0, 0), (0, padded - share)))

    pieces = jnp.concatenate([shares(gate_weight), shares(up_weight)], axis=2)
    length = 2 * block_input.shape[0]
    cosine, sine = rope_tables(length, HD)
    still, none = jnp.ones((length, HD), f32), jnp.zeros((length, HD), f32)
    twice = jnp.concatenate([cosine] * 4, axis=1)
    signed = jnp.concatenate([-sine, sine] * 2, axis=1)
    tables = jnp.stack(
        [
            twice,
            signed,
            jnp.concatenate([twice[:, :HD], still], axis=1),
            jnp.concatenate([signed[:, :HD], none], axis=1),
        ]
    )
    (
        gains_rows,
        narrow_full,
        out_full,
        wide,
        downs,
        cot_rows,
        ffn_rows,
        normed_one,
        heads,
        attn_rows,
        residual,
    ) = front(
        gains, narrow, output_weight, pieces, down_weight, block_input, output_cotangent, tables
    )
    cot_rows = cot_rows.reshape(-1, width)
    ffn_rows = ffn_rows.reshape(-1, width)
    wide_full = wide.reshape(width, 2 * padded)
    down_share = downs.reshape(share, width)
    half = block_input.shape[0]

    hidden, back_sum, wide_grad, factors, wide_factors = units(
        ffn_rows, cot_rows, wide_full, down_share, gains_rows, padded
    )
    back_sum = back_sum.reshape(GROUP, half, width)
    back_out = [narrowed(back_sum[key], factors[0, 0, :1]) for key in range(1, GROUP)]
    back_in = exchanged(back_out, partner)

    wide_grad = after(wide_grad.reshape(lines, GROUP * rows, 2 * padded), *back_out)
    wide_out = messages_of(wide_grad, wide_factors[0, :1], own)
    wide_in = exchanged(wide_out, across)
    hidden = after(hidden, *wide_out)
    down_grad, forth_sum = grads(cot_rows, hidden, down_share)
    down_grad = down_grad.reshape(lines, unit_rows, width)
    down_out = messages_of(down_grad, factors[1, 0, :1], own)
    down_in = exchanged(down_out, across)

    back_in = after(back_in, *down_out)
    second_cot = added(back_sum[0], back_in, factors[0, 1, :1])
    residual_cot, mix, out_grad, sums, out_factors = turn(
        second_cot, residual, gains_rows, output_cotangent, attn_rows, out_full
    )
    out_grad = out_grad.reshape(lines, GROUP, -1, width)
    out_out = group_messages(out_grad, place, out_factors[0, :1], out_factors[2])
    out_in = exchanged(out_out, partner)
    residual_cot = after(residual_cot, *out_out)
    input_grad, narrow_grad, narrow_factors = rear(
        residual_cot,
        mix,
        sums,
        gains_rows,
        block_input,
        heads,
        attn_rows,
        narrow_full,
        normed_one,
        tables,
    )
    narrow_grad = narrow_grad.reshape(lines, GROUP, -1, cols)
    narrow_out = group_messages(narrow_grad, place, narrow_factors[0, :1], narrow_factors[2])
    narrow_in = exchanged(narrow_out, partner)

    forth_sum = after(forth_sum.reshape(GROUP, half, width), *narrow_out)
    forth_out = [narrowed(forth_sum[key], factors[2, 0, :1]) for key in range(1, GROUP)]
    forth_in = exchanged(forth_out, partner)
    out_in = after(out_in, *forth_out)
    out_undos = [undo_of(message) for message in out_in]
    out_sum = lax.dynamic_index_in_dim(out_grad, place, 1, keepdims=False)
    out_sum = added_noted(out_sum, out_in, out_undos)
    out_line = line_messages(out_sum, raised(out_factors[1, :1], out_undos), own)
    out_line_in = exchanged(out_line, across)
    wide_in = after(wide_in, *out_line)
    wide_undo = wide_factors[1, :1]
    wide_own = added(lax.dynamic_index_in_dim(wide_grad, own, 0, keepdims=False), wide_in, wide_undo)
    wide_own = wide_own.reshape(GROUP, rows, 2 * padded)
    share_out = messages_of(wide_own, 0.25 * wide_factors[0, :1], place)
    share_in = exchanged(share_out, partner)
    narrow_in = after(narrow_in, *share_out)
    narrow_undos = [undo_of(message) for message in narrow_in]
    narrow_sum = lax.dynamic_index_in_dim(narrow_grad, place, 1, keepdims=False)
    narrow_sum = added_noted(narrow_sum, narrow_in, narrow_undos)
    narrow_line = line_messages(narrow_sum, raised(narrow_factors[1, :1], narrow_undos), own)
    narrow_line_in = exchanged(narrow_line, across)
    forth_in = after(forth_in, *narrow_line)
    block_output = (residual + added(forth_sum[0], forth_in, factors[2, 1, :1])).astype(bf16)
    share_in = after(share_in, block_output)
    pieces = [lax.dynamic_index_in_dim(wide_own, place, 0, keepdims=False)]
    pieces += [message.astype(f32) * (4.0 * wide_undo) for message in share_in]
    gate_own, up_own = unshare(jnp.stack(pieces), share, lines)
    down_in = after(down_in, gate_own, up_own)
    down_own = lax.dynamic_index_in_dim(down_grad, own, 0, keepdims=False)
    down_own = added(down_own, down_in, factors[1, 1, :1])
    out_line_in = after(out_line_in, down_own)
    out_own = added_noted(
        lax.dynamic_index_in_dim(out_sum, own, 0, keepdims=False),
        out_line_in,
        [undo_of(message) for message in out_line_in],
    )
    narrow_line_in = after(narrow_line_in, out_own)
    narrow_own = added_noted(
        lax.dynamic_index_in_dim(narrow_sum, own, 0, keepdims=False),
        narrow_line_in,
        [undo_of(message) for message in narrow_line_in],
    )
    return (
        block_output,
        input_grad,
        narrow_own[rows, :rows],
        narrow_own[:rows, :query_cols],
        narrow_own[:rows, query_cols : query_cols + key_cols],
        narrow_own[:rows, query_cols + key_cols :],
        out_own,
        narrow_own[rows, LANES : LANES + rows],
        gate_own,
        up_own,
        down_own,
    )


def solution(mesh):
    placed = (
        P(("dp", "mp"), None),
        P("dp"),
        P("dp", "mp"),
        P("dp", "mp"),
        P("dp", "mp"),
        P(("mp", "dp"), None),
        P("dp"),
        P("dp", "mp"),
        P("dp", "mp"),
        P(("mp", "dp"), None),
        P(("dp", "mp"), None),
    )
    members = mesh.shape["dp"]
    fits = mesh.shape["mp"] == 2 and members in (2 * GROUP, 4 * GROUP)
    return jax.shard_map(
        grouped_shards if fits else plain_shards,
        mesh=mesh,
        in_specs=placed,
        out_specs=(
            P(("dp", "mp"), None),
            P(("dp", "mp"), None),
            P("dp"),
            P("dp", "mp"),
            P("dp", "mp"),
            P("dp", "mp"),
            P(("mp", "dp"), None),
            P("dp"),
            P("dp", "mp"),
            P("dp", "mp"),
            P(("mp", "dp"), None),
        ),
        check_vma=False,
    )
```

profile of v0, /device:TPU:10, one launch (start us, length us, event | category | flops | bytes accessed | tf_op | source)
XLA Modules:
  0.0 321.1 jit_solution(17782935400539944679)
XLA Ops:
  0.7 0.9 copy.38
  2.4 1.2 copy.42
  6.3 93.5 %front.1 = (f32[16,1792]{1,0:T(8,128)S(1)}, bf16[1792,640]{1,0:T(8,128)(2,1)S(1)}, bf16[512,1792]{1,0:T(8,128)(2,1)S(1)}, bf16[4,4,112,768]{3,2,1,0:T(8,128)(2,1...) custom-call(bf16[8,128]{1,0:T(8,128)(2,1)S(1)} %fusion.53.gains, ...), custom_call_target="tpu_custom_call" | custom-call | tf_op jit(solution)/shard_map/front/pallas_call | solution.py:820
  99.8 0.9 copy-done.4
  100.7 1.4 copy-done.15
  102.1 1.2 copy-done.17
  104.0 25.9 %units.1 = (bf16[1024,384]{1,0:T(8,128)(2,1)S(1)}, f32[512,1792]{1,0:T(8,128)}, f32[1792,768]{1,0:T(8,128)}, f32[3,3,8,1792]{3,2,1,0:T(8,128)S(1)}, f32[3,8,768]{2,1,0:T(8,128)S(1)}) custom-call(bf16[1024,1792]{1,0:T(8,128)(2,1)} %bitcast.225, bf16[1024,1792]{1,0:T(8,128)(2,1)} %bitcast.204, bf16[1792,768]{1,0:T(8,128)(2,1)S(1)} %bitcast.206, ...), custom_call_target="tpu_custom_call" | custom-call | flops 10000000000 | bytes 20000000 | tf_op jit(solution)/shard_map/units/pallas_call | solution.py:1092
  130.1 3.1 multiply_convert_fusion
  133.8 1.5 collective-permute-start.1
  135.3 1.3 collective-permute-start.2
  136.7 3.7 %fusion = (f16[448,768]{1,0:T(8,128)(2,1)}, f16[448,768]{1,0:T(8,128)(2,1)}, f16[448,768]{1,0:T(8,128)(2,1)}) fusion(f32[4,448,768]{2,1,0:T(8,128)} %bitcast.209, s32[]{:T(128)S(6)} %select_n.59, f32[768]{0:T(1024)S(1)} %get-tuple-element.179, s32[]{:T(128)S(6)} %select_n.58, s32[]{:T(128)S(6)} %select_n.57), kind=kLoop, calls=%fused_computation.5 | loop fusion | flops 2064384 | bytes 6196236 | tf_op jit(solution)/shard_map/convert_element_type | solution.py:289
  140.4 1.5 collective-permute-start.9
  143.0 2.0 copy-done.14
  145.0 1.3 copy-done.20
  146.3 1.1 copy-done.30
  147.5 9.0 %grads.1 = (f32[352,1792]{1,0:T(8,128)S(1)}, f32[512,1792]{1,0:T(8,128)S(1)}) custom-call(bf16[1024,1792]{1,0:T(8,128)(2,1)S(1)} %bitcast.205, bf16[1024,384]{1,0:T(8,128)(2,1)S(1)} %copy-done.30, bf16[352,1792]{1,0:T(8,128)(2,1)S(1)} %bitcast.208), custom_call_target="tpu_custom_call" | custom-call | flops 10000000000 | bytes 20000000 | tf_op jit(solution)/shard_map/grads/pallas_call | solution.py:1190
  156.5 1.9 copy-done.2
  158.3 1.0 fusion.21
  159.4 2.0 multiply_add_fusion.second_cot
  161.9 6.2 %turn.1 = (f32[128,1792]{1,0:T(8,128)S(1)}, bf16[256,512]{1,0:T(8,128)(2,1)S(1)}, f32[512,1792]{1,0:T(8,128)S(1)}, f32[8,1792]{1,0:T(8,128)S(1)}, f32[3,8,1792]{2,1,0:T(8,128)S(1)}) custom-call(f32[128,1792]{1,0:T(8,128)S(1)} %multiply_add_fusion.second_cot, f32[128,1792]{1,0:T(8,128)S(1)} %copy-done.5, f32[16,1792]{1,0:T(8,128)S(1)} %copy-done.28, ...), custom_call_target="tpu_custom_call" | custom-call | flops 10000000000 | bytes 20000000 | tf_op jit(solution)/shard_map/turn/pallas_call | solution.py:1339
  168.4 1.5 copy-done.1
  172.2 15.9 %rear.1 = (f32[128,1792]{1,0:T(8,128)S(1)}, f32[16,120,640]{2,1,0:T(8,128)S(1)}, f32[3,8,640]{2,1,0:T(8,128)S(1)}) custom-call(f32[128,1792]{1,0:T(8,128)S(1)} %get-tuple-element.97.residual_cot, bf16[256,512]{1,0:T(8,128)(2,1)S(1)} %get-tuple-element.98.mix, f32[8,1792]{1,0:T(8,128)S(1)} %get-tuple-element.99.sums, f32[16,1792]{1,0:T(8,128)S(1)} %copy-done.28, ...), custom_call_target="tpu_custom_call" | custom-call | flops 10000000000 | bytes 20000000 | tf_op jit(solution)/shard_map/rear/pallas_call | solution.py:1537
  189.4 1.5 collective-permute-start.13
  190.9 1.3 collective-permute-start.14
  192.9 1.5 pad_maximum_fusion.1
  194.4 1.2 copy-done.3
  195.6 1.2 fusion.12
  196.7 6.0 %collective-permute-done.12 = f16[136,1792]{1,0:T(8,128)(2,1)S(1)} collective-permute-done((f16[136,1792]{1,0:T(8,128)(2,1)S(1)}, f16[136,1792]{1,0:T(8,128)(2,1)S(1)}, u32[]{:S(2)}, u32[]{:S(2)}) %collective-permute-start.12) | collective-permute-done | bytes 487456 | tf_op jit(solution)/shard_map/ppermute | solution.py:276
  202.8 1.5 collective-permute-start.11
  204.3 8.4 %collective-permute-done.13 = f16[136,1792]{1,0:T(8,128)(2,1)S(1)} collective-permute-done((f16[136,1792]{1,0:T(8,128)(2,1)S(1)}, f16[136,1792]{1,0:T(8,128)(2,1)S(1)}, u32[]{:S(2)}, u32[]{:S(2)}) %collective-permute-start.13) | collective-permute-done | bytes 487456 | tf_op jit(solution)/shard_map/ppermute | solution.py:276
  212.6 1.8 collective-permute-start.21
  214.4 1.1 collective-permute-start.22
  215.6 1.0 convert_multiply_fusion.3
  216.6 1.0 convert_multiply_fusion.4
  217.7 1.0 convert_multiply_fusion.5
  219.4 2.2 fusion.11
  222.5 1.4 collective-permute-start.6
  224.7 17.7 %collective-permute-done.11 = f16[448,768]{1,0:T(8,128)(2,1)} collective-permute-done((f16[448,768]{1,0:T(8,128)(2,1)}, f16[448,768]{1,0:T(8,128)(2,1)}, u32[]{:S(2)}, u32[]{:S(2)}) %collective-permute-start.11) | collective-permute-done | bytes 688160 | tf_op jit(solution)/shard_map/ppermute | solution.py:281
  242.4 1.6 collective-permute-start.8
  244.0 2.3 bitcast_add_fusion
  248.4 1.3 collective-permute-start.4
  249.7 10.5 %collective-permute-done.8 = f16[488,640]{1,0:T(8,128)(2,1)S(1)} collective-permute-done((f16[488,640]{1,0:T(8,128)(2,1)S(1)}, f16[488,640]{1,0:T(8,128)(2,1)S(1)}, u32[]{:S(2)}, u32[]{:S(2)}) %collective-permute-start.8) | collective-permute-done | bytes 624672 | tf_op jit(solution)/shard_map/ppermute | solution.py:276
  260.2 1.6 collective-permute-start.5
  262.8 2.6 fusion.6
  265.5 1.3 fusion.29
  267.7 1.7 collective-permute-done.3
  269.4 1.5 collective-permute-start.24
  271.4 7.1 %collective-permute-done.5 = f16[128,1792]{1,0:T(8,128)(2,1)} collective-permute-done((f16[128,1792]{1,0:T(8,128)(2,1)}, f16[128,1792]{1,0:T(8,128)(2,1)}, u32[]{:S(2)}, u32[]{:S(2)}) %collective-permute-start.5) | collective-permute-done | bytes 458784 | tf_op jit(solution)/shard_map/ppermute | solution.py:276
  278.5 1.6 collective-permute-start.26
  280.1 2.6 fusion.16
  282.7 1.8 collective-permute-start.23
  284.8 1.4 collective-permute-start.19
  286.3 1.2 pad_maximum_fusion.pieces
  287.6 2.9 unshare.1
  290.5 1.8 collective-permute-start.20
  292.3 1.2 collective-permute-start.15
  293.5 11.0 %collective-permute-done.23 = f16[88,1792]{1,0:T(8,128)(2,1)S(1)} collective-permute-done((f16[88,1792]{1,0:T(8,128)(2,1)}, f16[88,1792]{1,0:T(8,128)(2,1)S(1)}, u32[]{:S(2)}, u32[]{:S(2)}) %collective-permute-start.23) | collective-permute-done | bytes 315424 | tf_op jit(solution)/shard_map/ppermute | solution.py:281
  304.5 2.1 bitcast_add_fusion.4
  307.0 4.1 %collective-permute-done.20 = f16[40,1792]{1,0:T(8,128)(2,1)S(1)} collective-permute-done((f16[40,1792]{1,0:T(8,128)(2,1)}, f16[40,1792]{1,0:T(8,128)(2,1)S(1)}, u32[]{:S(2)}, u32[]{:S(2)}) %collective-permute-start.20) | collective-permute-done | bytes 143392 | tf_op jit(solution)/shard_map/ppermute | solution.py:281
  311.1 1.8 fusion.33
  312.9 1.0 collective-permute-done.16
  313.9 2.4 collective-permute-done.17
  316.4 1.1 fusion.28
  320.1 0.9 copy.50
  (177 shorter events, 21.5 us)
Async XLA Ops:
  0.6 3.2 copy-start.36
  5.0 1.3 copy-start.13
  100.7 1.4 copy-start.15
  102.1 1.2 copy-start.17
  104.0 25.9 %copy-start.19 = (bf16[4,88,1792]{2,1,0:T(8,128)(2,1)}, bf16[4,88,1792]{2,1,0:T(8,128)(2,1)S(1)}, u32[]{:S(2)}) copy-start(bf16[4,88,1792]{2,1,0:T(8,128)(2,1)S(1)} %get-tuple-element.78) | copy-start | bytes 3784708
  104.0 25.9 %copy-start.21 = (bf16[256,1792]{1,0:T(8,128)(2,1)}, bf16[256,1792]{1,0:T(8,128)(2,1)S(1)}, u32[]{:S(2)}) copy-start(bf16[256,1792]{1,0:T(8,128)(2,1)S(1)} %get-tuple-element.102.normed) | copy-start | bytes 2752516
  104.0 26.0 %copy-start.23 = (bf16[256,640]{1,0:T(8,128)(2,1)}, bf16[256,640]{1,0:T(8,128)(2,1)S(1)}, u32[]{:S(2)}) copy-start(bf16[256,640]{1,0:T(8,128)(2,1)S(1)} %get-tuple-element.100.heads) | copy-start | bytes 983044
  104.0 26.0 %copy-start.27 = (f32[16,1792]{1,0:T(8,128)}, f32[16,1792]{1,0:T(8,128)S(1)}, u32[]{:S(2)}) copy-start(f32[16,1792]{1,0:T(8,128)S(1)} %get-tuple-element.79.gains) | copy-start | bytes 344068
  130.0 3.2 copy-start.29
  133.2 26.2 %collective-permute-start = (f16[128,1792]{1,0:T(8,128)(2,1)}, f16[128,1792]{1,0:T(8,128)(2,1)}, u32[]{:S(2)}, u32[]{:S(2)}) collective-permute-start(f16[128,1792]{1,0:T(8,128)(2,1)} %get-tuple-element.193), channel_id=1, source_target_pairs={{0,2},{2,0},{4,6},{6,4},{8,10},{10,8},{12,14},{14,12},{16,18},{18,... | collective-permute-start | bytes 1376264 | tf_op jit(solution)/shard_map/ppermute | solution.py:276
  133.8 25.5 %collective-permute-start.1 = (f16[128,1792]{1,0:T(8,128)(2,1)}, f16[128,1792]{1,0:T(8,128)(2,1)}, u32[]{:S(2)}, u32[]{:S(2)}) collective-permute-start(f16[128,1792]{1,0:T(8,128)(2,1)} %get-tuple-element.192), channel_id=1, source_target_pairs={{0,4},{2,6},{4,0},{6,2},{8,12},{10,14},{12,8},{14,10},{16,20},{18,... | collective-permute-start | bytes 1376264 | tf_op jit(solution)/shard_map/ppermute | solution.py:276
  135.3 24.0 %collective-permute-start.2 = (f16[128,1792]{1,0:T(8,128)(2,1)}, f16[128,1792]{1,0:T(8,128)(2,1)}, u32[]{:S(2)}, u32[]{:S(2)}) collective-permute-start(f16[128,1792]{1,0:T(8,128)(2,1)} %get-tuple-element.191), channel_id=1, source_target_pairs={{0,6},{2,4},{4,2},{6,0},{8,14},{10,12},{12,10},{14,8},{16,22},{18,... | collective-permute-start | bytes 1376264 | tf_op jit(solution)/shard_map/ppermute | solution.py:276
  140.4 82.2 %collective-permute-start.9 = (f16[448,768]{1,0:T(8,128)(2,1)}, f16[448,768]{1,0:T(8,128)(2,1)}, u32[]{:S(2)}, u32[]{:S(2)}) collective-permute-start(f16[448,768]{1,0:T(8,128)(2,1)} %get-tuple-element.184), channel_id=1, source_target_pairs={{0,8},{2,10},{4,12},{6,14},{8,0},{10,2},{12,4},{14,6},{16,24},{18,... | collective-permute-start | bytes 2064392 | tf_op jit(solution)/shard_map/ppermute | solution.py:281
  141.8 82.1 %collective-permute-start.10 = (f16[448,768]{1,0:T(8,128)(2,1)}, f16[448,768]{1,0:T(8,128)(2,1)}, u32[]{:S(2)}, u32[]{:S(2)}) collective-permute-start(f16[448,768]{1,0:T(8,128)(2,1)} %get-tuple-element.183), channel_id=1, source_target_pairs={{0,16},{2,18},{4,20},{6,22},{8,24},{10,26},{12,28},{14,30},{16,0},... | collective-permute-start | bytes 2064392 | tf_op jit(solution)/shard_map/ppermute | solution.py:281
  143.0 2.0 copy-start.14
  145.0 1.3 copy-start.20
  156.4 1.9 copy-start.2
  159.4 2.0 copy-start.5
  159.4 2.5 copy-start.18
  159.4 2.5 copy-start.26
  159.4 2.5 copy-start.28
  168.1 1.8 copy-start.1
  169.9 1.2 copy-start.24
  170.2 1.9 copy-start.16
  188.1 4.4 %copy-start = (f32[16,120,640]{2,1,0:T(8,128)}, f32[16,120,640]{2,1,0:T(8,128)S(1)}, u32[]{:S(2)}) copy-start(f32[16,120,640]{2,1,0:T(8,128)S(1)} %get-tuple-element.103) | copy-start | bytes 14745604
  188.1 4.4 %copy-start.7 = (f32[128,1792]{1,0:T(8,128)}, f32[128,1792]{1,0:T(8,128)S(1)}, u32[]{:S(2)}) copy-start(f32[128,1792]{1,0:T(8,128)S(1)} %get-tuple-element.255) | copy-start | bytes 2752516
  188.8 14.0 %collective-permute-start.12 = (f16[136,1792]{1,0:T(8,128)(2,1)S(1)}, f16[136,1792]{1,0:T(8,128)(2,1)S(1)}, u32[]{:S(2)}, u32[]{:S(2)}) collective-permute-start(f16[136,1792]{1,0:T(8,128)(2,1)S(1)} %get-tuple-element.222), channel_id=1, source_target_pairs={{0,2},{2,0},{4,6},{6,4},{8,10},{10,8},{12,14},{14,12},{16,18},{18,... | collective-permute-start | bytes 1462280 | tf_op jit(solution)/shard_map/ppermute | solution.py:276
  189.4 23.2 %collective-permute-start.13 = (f16[136,1792]{1,0:T(8,128)(2,1)S(1)}, f16[136,1792]{1,0:T(8,128)(2,1)S(1)}, u32[]{:S(2)}, u32[]{:S(2)}) collective-permute-start(f16[136,1792]{1,0:T(8,128)(2,1)S(1)} %get-tuple-element.221), channel_id=1, source_target_pairs={{0,4},{2,6},{4,0},{6,2},{8,12},{10,14},{12,8},{14,10},{16,20},{18,... | collective-permute-start | bytes 1462280 | tf_op jit(solution)/shard_map/ppermute | solution.py:276
  190.9 23.5 %collective-permute-start.14 = (f16[136,1792]{1,0:T(8,128)(2,1)S(1)}, f16[136,1792]{1,0:T(8,128)(2,1)S(1)}, u32[]{:S(2)}, u32[]{:S(2)}) collective-permute-start(f16[136,1792]{1,0:T(8,128)(2,1)S(1)} %get-tuple-element.220), channel_id=1, source_target_pairs={{0,6},{2,4},{4,2},{6,0},{8,14},{10,12},{12,10},{14,8},{16,22},{18,... | collective-permute-start | bytes 1462280 | tf_op jit(solution)/shard_map/ppermute | solution.py:276
  192.9 2.7 copy-start.3
  202.8 39.6 %collective-permute-start.11 = (f16[448,768]{1,0:T(8,128)(2,1)}, f16[448,768]{1,0:T(8,128)(2,1)}, u32[]{:S(2)}, u32[]{:S(2)}) collective-permute-start(f16[448,768]{1,0:T(8,128)(2,1)} %get-tuple-element.182), channel_id=1, source_target_pairs={{0,24},{2,26},{4,28},{6,30},{8,16},{10,18},{12,20},{14,22},{16,8},... | collective-permute-start | bytes 2064392 | tf_op jit(solution)/shard_map/ppermute | solution.py:281
  212.6 77.9 %collective-permute-start.21 = (f16[88,1792]{1,0:T(8,128)(2,1)}, f16[88,1792]{1,0:T(8,128)(2,1)}, u32[]{:S(2)}, u32[]{:S(2)}) collective-permute-start(f16[88,1792]{1,0:T(8,128)(2,1)} %get-tuple-element.199), channel_id=1, source_target_pairs={{0,8},{2,10},{4,12},{6,14},{8,0},{10,2},{12,4},{14,6},{16,24},{18,... | collective-permute-start | bytes 946184 | tf_op jit(solution)/shard_map/ppermute | solution.py:281
  214.4 77.9 %collective-permute-start.22 = (f16[88,1792]{1,0:T(8,128)(2,1)}, f16[88,1792]{1,0:T(8,128)(2,1)}, u32[]{:S(2)}, u32[]{:S(2)}) collective-permute-start(f16[88,1792]{1,0:T(8,128)(2,1)} %get-tuple-element.198), channel_id=1, source_target_pairs={{0,16},{2,18},{4,20},{6,22},{8,24},{10,26},{12,28},{14,30},{16,0},... | collective-permute-start | bytes 946184 | tf_op jit(solution)/shard_map/ppermute | solution.py:281
  219.4 2.3 copy-start.44
  219.4 3.2 copy-start.35
  221.6 24.6 %copy-start.31 = (f32[4,32,1792]{2,1,0:T(8,128)}, f32[4,32,1792]{2,1,0:T(8,128)S(1)}, u32[]{:S(2)}) copy-start(f32[4,32,1792]{2,1,0:T(8,128)S(1)} %fusion.11) | copy-start | bytes 2752516
  221.6 2.3 copy-start.34
  221.6 20.7 %copy-start.33 = (f16[488,640]{1,0:T(8,128)(2,1)S(1)}, f16[488,640]{1,0:T(8,128)(2,1)}, u32[]{:S(2)}) copy-start(f16[488,640]{1,0:T(8,128)(2,1)} %get-tuple-element.226) | copy-start | bytes 1873924
  222.5 25.3 %collective-permute-start.6 = (f16[488,640]{1,0:T(8,128)(2,1)S(1)}, f16[488,640]{1,0:T(8,128)(2,1)S(1)}, u32[]{:S(2)}, u32[]{:S(2)}) collective-permute-start(f16[488,640]{1,0:T(8,128)(2,1)S(1)} %copy-done.35), channel_id=1, source_target_pairs={{0,2},{2,0},{4,6},{6,4},{8,10},{10,8},{12,14},{14,12},{16,18},{18,... | collective-permute-start | bytes 1873928 | tf_op jit(solution)/shard_map/ppermute | solution.py:276
  223.9 24.5 %collective-permute-start.7 = (f16[488,640]{1,0:T(8,128)(2,1)S(1)}, f16[488,640]{1,0:T(8,128)(2,1)S(1)}, u32[]{:S(2)}, u32[]{:S(2)}) collective-permute-start(f16[488,640]{1,0:T(8,128)(2,1)S(1)} %copy-done.34), channel_id=1, source_target_pairs={{0,4},{2,6},{4,0},{6,2},{8,12},{10,14},{12,8},{14,10},{16,20},{18,... | collective-permute-start | bytes 1873928 | tf_op jit(solution)/shard_map/ppermute | solution.py:276
  242.4 17.9 %collective-permute-start.8 = (f16[488,640]{1,0:T(8,128)(2,1)S(1)}, f16[488,640]{1,0:T(8,128)(2,1)S(1)}, u32[]{:S(2)}, u32[]{:S(2)}) collective-permute-start(f16[488,640]{1,0:T(8,128)(2,1)S(1)} %copy-done.33), channel_id=1, source_target_pairs={{0,6},{2,4},{4,2},{6,0},{8,14},{10,12},{12,10},{14,8},{16,22},{18,... | collective-permute-start | bytes 1873928 | tf_op jit(solution)/shard_map/ppermute | solution.py:276
  244.0 3.1 copy-start.45
  247.8 21.6 %collective-permute-start.3 = (f16[128,1792]{1,0:T(8,128)(2,1)}, f16[128,1792]{1,0:T(8,128)(2,1)}, u32[]{:S(2)}, u32[]{:S(2)}) collective-permute-start(f16[128,1792]{1,0:T(8,128)(2,1)} %get-tuple-element.190), channel_id=1, source_target_pairs={{0,2},{2,0},{4,6},{6,4},{8,10},{10,8},{12,14},{14,12},{16,18},{18,... | collective-permute-start | bytes 1376264 | tf_op jit(solution)/shard_map/ppermute | solution.py:276
  248.4 22.5 %collective-permute-start.4 = (f16[128,1792]{1,0:T(8,128)(2,1)}, f16[128,1792]{1,0:T(8,128)(2,1)}, u32[]{:S(2)}, u32[]{:S(2)}) collective-permute-start(f16[128,1792]{1,0:T(8,128)(2,1)} %get-tuple-element.189), channel_id=1, source_target_pairs={{0,4},{2,6},{4,0},{6,2},{8,12},{10,14},{12,8},{14,10},{16,20},{18,... | collective-permute-start | bytes 1376264 | tf_op jit(solution)/shard_map/ppermute | solution.py:276
  260.2 18.3 %collective-permute-start.5 = (f16[128,1792]{1,0:T(8,128)(2,1)}, f16[128,1792]{1,0:T(8,128)(2,1)}, u32[]{:S(2)}, u32[]{:S(2)}) collective-permute-start(f16[128,1792]{1,0:T(8,128)(2,1)} %get-tuple-element.188), channel_id=1, source_target_pairs={{0,6},{2,4},{4,2},{6,0},{8,14},{10,12},{12,10},{14,8},{16,22},{18,... | collective-permute-start | bytes 1376264 | tf_op jit(solution)/shard_map/ppermute | solution.py:276
  265.4 14.7 %copy-start.6 = (f32[128,1792]{1,0:T(8,128)S(1)}, f32[128,1792]{1,0:T(8,128)}, u32[]{:S(2)}) copy-start(f32[128,1792]{1,0:T(8,128)} %copy-done.4) | copy-start | bytes 2752516
  265.5 3.9 %copy-start.39 = (f16[112,768]{1,0:T(8,128)(2,1)S(1)}, f16[112,768]{1,0:T(8,128)(2,1)}, u32[]{:S(2)}) copy-start(f16[112,768]{1,0:T(8,128)(2,1)} %get-tuple-element.202) | copy-start | bytes 516100
  265.5 5.4 %copy-start.38 = (f16[112,768]{1,0:T(8,128)(2,1)S(1)}, f16[112,768]{1,0:T(8,128)(2,1)}, u32[]{:S(2)}) copy-start(f16[112,768]{1,0:T(8,128)(2,1)} %get-tuple-element.201) | copy-start | bytes 516100
  265.5 13.0 %copy-start.37 = (f16[112,768]{1,0:T(8,128)(2,1)S(1)}, f16[112,768]{1,0:T(8,128)(2,1)}, u32[]{:S(2)}) copy-start(f16[112,768]{1,0:T(8,128)(2,1)} %get-tuple-element.200) | copy-start | bytes 516100
  269.4 13.3 %collective-permute-start.24 = (f16[112,768]{1,0:T(8,128)(2,1)S(1)}, f16[112,768]{1,0:T(8,128)(2,1)S(1)}, u32[]{:S(2)}, u32[]{:S(2)}) collective-permute-start(f16[112,768]{1,0:T(8,128)(2,1)S(1)} %copy-done.39), channel_id=1, source_target_pairs={{0,2},{2,0},{4,6},{6,4},{8,10},{10,8},{12,14},{14,12},{16,18},{18,... | collective-permute-start | bytes 516104 | tf_op jit(solution)/shard_map/ppermute | solution.py:276
  270.9 13.6 %collective-permute-start.25 = (f16[112,768]{1,0:T(8,128)(2,1)S(1)}, f16[112,768]{1,0:T(8,128)(2,1)S(1)}, u32[]{:S(2)}, u32[]{:S(2)}) collective-permute-start(f16[112,768]{1,0:T(8,128)(2,1)S(1)} %copy-done.38), channel_id=1, source_target_pairs={{0,4},{2,6},{4,0},{6,2},{8,12},{10,14},{12,8},{14,10},{16,20},{18,... | collective-permute-start | bytes 516104 | tf_op jit(solution)/shard_map/ppermute | solution.py:276
  278.5 6.3 %collective-permute-start.26 = (f16[112,768]{1,0:T(8,128)(2,1)S(1)}, f16[112,768]{1,0:T(8,128)(2,1)S(1)}, u32[]{:S(2)}, u32[]{:S(2)}) collective-permute-start(f16[112,768]{1,0:T(8,128)(2,1)S(1)} %copy-done.37), channel_id=1, source_target_pairs={{0,6},{2,4},{4,2},{6,0},{8,14},{10,12},{12,10},{14,8},{16,22},{18,... | collective-permute-start | bytes 516104 | tf_op jit(solution)/shard_map/ppermute | solution.py:276
  282.7 3.6 %copy-start.32 = (f32[1,112,768]{2,1,0:T(8,128)S(1)}, f32[1,112,768]{2,1,0:T(8,128)}, u32[]{:S(2)}) copy-start(f32[1,112,768]{2,1,0:T(8,128)} %constant_dynamic-slice_fusion) | copy-start | bytes 1032196
  282.7 21.7 %collective-permute-start.23 = (f16[88,1792]{1,0:T(8,128)(2,1)}, f16[88,1792]{1,0:T(8,128)(2,1)S(1)}, u32[]{:S(2)}, u32[]{:S(2)}) collective-permute-start(f16[88,1792]{1,0:T(8,128)(2,1)} %get-tuple-element.197), channel_id=1, source_target_pairs={{0,24},{2,26},{4,28},{6,30},{8,16},{10,18},{12,20},{14,22},{16,8},... | collective-permute-start | bytes 946184 | tf_op jit(solution)/shard_map/ppermute | solution.py:281
  284.5 22.0 %collective-permute-start.18 = (f16[40,1792]{1,0:T(8,128)(2,1)}, f16[40,1792]{1,0:T(8,128)(2,1)S(1)}, u32[]{:S(2)}, u32[]{:S(2)}) collective-permute-start(f16[40,1792]{1,0:T(8,128)(2,1)} %get-tuple-element.219), channel_id=1, source_target_pairs={{0,8},{2,10},{4,12},{6,14},{8,0},{10,2},{12,4},{14,6},{16,24},{18,... | collective-permute-start | bytes 430088 | tf_op jit(solution)/shard_map/ppermute | solution.py:281
  284.8 22.2 %collective-permute-start.19 = (f16[40,1792]{1,0:T(8,128)(2,1)}, f16[40,1792]{1,0:T(8,128)(2,1)S(1)}, u32[]{:S(2)}, u32[]{:S(2)}) collective-permute-start(f16[40,1792]{1,0:T(8,128)(2,1)} %get-tuple-element.218), channel_id=1, source_target_pairs={{0,16},{2,18},{4,20},{6,22},{8,24},{10,26},{12,28},{14,30},{16,0},... | collective-permute-start | bytes 430088 | tf_op jit(solution)/shard_map/ppermute | solution.py:281
  286.3 6.0 %copy-start.42 = (f16[128,640]{1,0:T(8,128)(2,1)S(1)}, f16[128,640]{1,0:T(8,128)(2,1)}, u32[]{:S(2)}) copy-start(f16[128,640]{1,0:T(8,128)(2,1)} %get-tuple-element.225) | copy-start | bytes 491524
  286.3 18.1 %copy-start.41 = (f16[128,640]{1,0:T(8,128)(2,1)S(1)}, f16[128,640]{1,0:T(8,128)(2,1)}, u32[]{:S(2)}) copy-start(f16[128,640]{1,0:T(8,128)(2,1)} %get-tuple-element.224) | copy-start | bytes 491524
  290.5 16.1 %copy-start.40 = (f16[128,640]{1,0:T(8,128)(2,1)S(1)}, f16[128,640]{1,0:T(8,128)(2,1)}, u32[]{:S(2)}) copy-start(f16[128,640]{1,0:T(8,128)(2,1)} %get-tuple-element.223) | copy-start | bytes 491524
  290.5 20.5 %collective-permute-start.20 = (f16[40,1792]{1,0:T(8,128)(2,1)}, f16[40,1792]{1,0:T(8,128)(2,1)S(1)}, u32[]{:S(2)}, u32[]{:S(2)}) collective-permute-start(f16[40,1792]{1,0:T(8,128)(2,1)} %get-tuple-element.217), channel_id=1, source_target_pairs={{0,24},{2,26},{4,28},{6,30},{8,16},{10,18},{12,20},{14,22},{16,8},... | collective-permute-start | bytes 430088 | tf_op jit(solution)/shard_map/ppermute | solution.py:281
  292.3 20.6 %collective-permute-start.15 = (f16[128,640]{1,0:T(8,128)(2,1)S(1)}, f16[128,640]{1,0:T(8,128)(2,1)S(1)}, u32[]{:S(2)}, u32[]{:S(2)}) collective-permute-start(f16[128,640]{1,0:T(8,128)(2,1)S(1)} %copy-done.42), channel_id=1, source_target_pairs={{0,8},{2,10},{4,12},{6,14},{8,0},{10,2},{12,4},{14,6},{16,24},{18,... | collective-permute-start | bytes 491528 | tf_op jit(solution)/shard_map/ppermute | solution.py:281
  304.5 9.4 %collective-permute-start.16 = (f16[128,640]{1,0:T(8,128)(2,1)S(1)}, f16[128,640]{1,0:T(8,128)(2,1)S(1)}, u32[]{:S(2)}, u32[]{:S(2)}) collective-permute-start(f16[128,640]{1,0:T(8,128)(2,1)S(1)} %copy-done.41), channel_id=1, source_target_pairs={{0,16},{2,18},{4,20},{6,22},{8,24},{10,26},{12,28},{14,30},{16,0},... | collective-permute-start | bytes 491528 | tf_op jit(solution)/shard_map/ppermute | solution.py:281
  306.5 9.8 %collective-permute-start.17 = (f16[128,640]{1,0:T(8,128)(2,1)S(1)}, f16[128,640]{1,0:T(8,128)(2,1)S(1)}, u32[]{:S(2)}, u32[]{:S(2)}) collective-permute-start(f16[128,640]{1,0:T(8,128)(2,1)S(1)} %copy-done.40), channel_id=1, source_target_pairs={{0,24},{2,26},{4,28},{6,30},{8,16},{10,18},{12,20},{14,22},{16,8},... | collective-permute-start | bytes 491528 | tf_op jit(solution)/shard_map/ppermute | solution.py:281
  311.1 9.0 %copy-start.8 = (f32[128,1792]{1,0:T(8,128)S(1)}, f32[128,1792]{1,0:T(8,128)}, u32[]{:S(2)}) copy-start(f32[128,1792]{1,0:T(8,128)} %copy-done.7) | copy-start | bytes 2752516
  (12 other events, 12.2 us)
where the time goes:
time: 323 us; the launch traced here: 321 us
  Pallas kernels  153 us (47%)
  waiting for transfers between devices  70.1 us (22%)
  other arithmetic  39.1 us (12%)
  starting transfers between devices  30.8 us (10%)
  local copies, waits for them, and re-layouts  26.3 us (8%)
    pallas_call x1, Pallas kernels, front(): pl.pallas_call(functools.partial(front_kernel, lines), out_shape=results,...  93.5 us
    ppermute x12, waiting for transfers between devices, across(): return lax.ppermute(values, 'dp', pairs)  36.1 us
    ppermute x15, waiting for transfers between devices, partner(): return lax.ppermute(values, 'dp', pairs)  34 us
    pallas_call x1, Pallas kernels, units(): pl.pallas_call(functools.partial(units_kernel, lines, share), out_shape=[...  25.9 us
    unnamed x105, local copies, waits for them, and re-layouts  22.4 us
    ppermute x15, starting transfers between devices, partner(): return lax.ppermute(values, 'dp', pairs)  17.8 us
    pallas_call x1, Pallas kernels, rear(): pl.pallas_call(functools.partial(rear_kernel, lines, members), out_shape=...  15.9 us
    ppermute x12, starting transfers between devices, across(): return lax.ppermute(values, 'dp', pairs)  13 us
  transfers between devices with their start and end apart: 27, of which 11 were waited for; matrix products, arithmetic and copies ran while one was open for 11% of the time, Pallas kernels for 11%

commit v1 on v0

--- a/solution.py
+++ b/solution.py
@@ -333,15 +333,41 @@
 
 
 def added_noted(total, messages, undos):
+    shape, cols = total.shape, total.shape[-1]
+    total = total.reshape(-1, cols)
     for message, undo in zip(messages, undos):
-        total = total + (message[:-8].astype(jnp.float32) * undo).reshape(total.shape)
-    return total
+        total = total + message[:-8].astype(jnp.float32) * undo
+    return total.reshape(shape)
 
 
 def raised(undo, undos):
     for other in undos:
         undo = jnp.maximum(undo, other)
     return 4.0 * undo
+
+
+def line_halves(blocks, scale, undo):
+    rows, cols = blocks.shape[1:]
+    own = lax.axis_index("dp") // GROUP
+    high, low = own // 2, lax.rem(own, 2)
+    blocks = blocks.reshape(2, 2, rows, cols)
+    away = lax.dynamic_index_in_dim(blocks, 1 - low, 1, keepdims=False)
+    message = narrowed(away.reshape(2 * rows, cols), scale)
+    near = across(message, 1).reshape(2, rows, cols)
+    keep = lax.dynamic_index_in_dim(blocks, low, 1, keepdims=False)
+
+    def half(which, near):
+        part = lax.dynamic_index_in_dim(near, which, 0, keepdims=False).astype(jnp.float32)
+        return lax.dynamic_index_in_dim(keep, which, 0, keepdims=False) + part * undo
+
+    def second(near):
+        message = narrowed(half(1 - high, near), 0.5 * scale)
+        return message, across(message, 2)
+
+    def ended(near, far):
+        return half(high, near) + far.astype(jnp.float32) * (2.0 * undo)
+
+    return message, near, second, ended
 
 
 def exchanged(messages, exchange):
@@ -585,7 +611,8 @@
     gains,
     narrow,
     out,
-    pieces,
+    gate,
+    up,
     down,
     inputs,
     cots,
@@ -604,7 +631,8 @@
     gains_v,
     narrow_v,
     out_v,
-    piece_v,
+    pieces,
+    shard_v,
     down_v,
     seq_v,
     cot_v,
@@ -653,12 +681,13 @@
                 (out, slot(out_v, index)),
                 (inputs, half_of(seq_v, core)),
                 (tables, tables_v),
+                (gate, shard_v.at[0]),
+                (up, shard_v.at[1]),
             )
         )
     ]
     for load in loads:
         load.start()
-    staged.add(pieces.at[place], piece_v, wide.at[own, place])
     staged.add(down, down_v, downs.at[own])
     staged.add(cots, cot_v, cot_rows.at[0, 0])
     seat.greet()
@@ -681,11 +710,28 @@
             )
         for key in (first, second):
             wires.send(source, slot(target, index), block_sem.at[which, index], seat.mate(key))
+    wires.send(inputs, half_of(seq_v, core), seq_sem.at[0], seat.twin())
+    for load in loads[5:]:
+        load.wait()
+    share, unit_rows = down.shape[0] * lines, down.shape[0]
+    padded = pieces.shape[2] // 2
+    fill = jnp.zeros((count, padded - share), pieces.dtype)
+    for which in range(2):
+        shard = shard_v[which]
+        for other in range(GROUP):
+            parts = []
+            for at in range(lines):
+                first = at * share + other * unit_rows
+                parts.append(shard[:, first : first + unit_rows])
+            pieces[other, :, which * padded : (which + 1) * padded] = jnp.concatenate(
+                parts + [fill], axis=1
+            )
     for key in range(1, GROUP):
         wires.send(
             pieces.at[flipped(place, key)], wide.at[own, place], mix_sem.at[key], seat.mate(key)
         )
-    wires.send(inputs, half_of(seq_v, core), seq_sem.at[0], seat.twin())
+    placed = pltpu.make_async_copy(pieces.at[place], wide.at[own, place], load_sem.at[7])
+    placed.start()
     staged.forward()
     for hop in range(1, lines):
         for _, target, which, first, second in whole:
@@ -704,6 +750,7 @@
                 landed(target, which, block)
                 pass_on(target, which, block, seat.mate(second))
     staged.finish()
+    placed.wait()
     for key in range(1, GROUP):
         wires.arrived(wide.at[own, flipped(place, key)], mix_sem.at[key], seat.twin())
     ffn = ((wide, line_sem.at[0]), (downs, line_sem.at[1]))
@@ -717,7 +764,7 @@
                 landed(target, which, block, ok)
                 pass_on(target, which, block, seat.mate(second), ok)
     spread_own(wires, seat, cots, cot_rows, cot_sem)
-    for load in loads:
+    for load in loads[:5]:
         load.wait()
     wires.arrived(half_of(seq_v, 1 - core), seq_sem.at[0], seat.twin())
     for _, target, which, first, second in whole:
@@ -789,13 +836,15 @@
 
 
 ANY = pl.BlockSpec(memory_space=pl.ANY)
-
-
-def front(gains, narrow, out, pieces, down, inputs, cots, tables):
+HBM = pl.BlockSpec(memory_space=pltpu.HBM)
+
+
+def front(gains, narrow, out, gate, up, down, inputs, cots, tables, padded):
     members = lax.axis_size("dp")
     lines = members // GROUP
     bf16, f32 = gains.dtype, jnp.float32
-    sources = (gains, narrow, out, pieces, down, inputs, cots, tables)
+    sources = (gains, narrow, out, gate, up, down, inputs, cots, tables)
+    pieces = jax.ShapeDtypeStruct((GROUP, gate.shape[0], 2 * padded), bf16)
     _, cols = narrow.shape
     half, width = inputs.shape
     depth = members * out.shape[0]
@@ -821,12 +870,13 @@
         functools.partial(front_kernel, lines),
         out_shape=results,
         in_specs=[ANY] * len(sources),
-        out_specs=[ANY] * len(results),
+        out_specs=[HBM] * len(results),
         scratch_shapes=[
             vmem((members,) + gains.shape, bf16),
             vmem((width, cols), bf16),
             vmem((depth, width), bf16),
-            vmem(pieces.shape[1:], bf16),
+            vmem(pieces.shape, bf16),
+            vmem((2,) + gate.shape, bf16),
             vmem(down.shape, bf16),
             vmem((2 * half, width), bf16),
             vmem(cots.shape, bf16),
@@ -840,8 +890,8 @@
             vmem((half, width), f32),
             vmem((half, width), f32),
             vmem((half, width), bf16),
-            dma((6,)),
-            dma((5,)),
+            dma((4,)),
+            dma((8,)),
             dma((8,)),
             dma((sends,)),
             dma((whole, members)),
@@ -852,7 +902,7 @@
             dma((2,)),
         ],
         compiler_params=pltpu.CompilerParams(
-            collective_id=0, has_side_effects=True, vmem_limit_bytes=40 << 20
+            collective_id=0, has_side_effects=True, vmem_limit_bytes=60 << 20
         ),
         name="front",
     )(*sources)
@@ -954,6 +1004,7 @@
     gains,
     hidden_out,
     back_out,
+    away_out,
     wide_out,
     factors,
     wide_factors,
@@ -1058,8 +1109,6 @@
     moves.put(wide_grad_v, wide_out)
     for at in range(chunks):
         wires.arrived(come_v.at[pl.ds(at * CHUNK, CHUNK)], come_sem.at[at], seat.twin())
-    sum_up(near_v, come_v)
-    moves.put(near_v, back_out)
     bounds = take_bounds(
         wires, seat, mine_v.at[pl.ds(8, 8)], bounds_v, bound_sem, others[:-1], len(mates)
     )
@@ -1071,13 +1120,22 @@
             bound = jnp.maximum(bound, bounds_v[last, at : at + 1, :])
         put_scales(bound, factors_v.at[at])
     put_scales(bounds[3:4, : 2 * padded], wide_factors_v)
+    each = half // GROUP
+    sum_up(near_v.at[pl.ds(0, each)], come_v.at[pl.ds(0, each)])
+    moves.put(near_v.at[pl.ds(0, each)], back_out)
+
+    def scaled(at, carry):
+        span = pl.ds(pl.multiple_of(each + at * STEP, STEP), STEP)
+        near_v[span, :] = (near_v[span, :] + come_v[span, :]) * factors_v[0, 0, 0:1, :]
+        return carry
+
+    lax.fori_loop(0, (half - each) // STEP, scaled, 0)
+    for at in range(1, GROUP):
+        moves.put(near_v.at[pl.ds(at * each, each)], away_out.at[at - 1])
     moves.put(factors_v, factors)
     moves.put(wide_factors_v, wide_factors)
     moves.finish()
     wires.drain()
-
-
-HBM = pl.BlockSpec(memory_space=pltpu.HBM)
 
 
 def units(rows, cots, wide, down, gains, padded):
@@ -1093,13 +1151,14 @@
         functools.partial(units_kernel, lines, share),
         out_shape=[
             shape((count, padded), bf16),
-            shape((half, width), f32),
+            shape((half // GROUP, width), f32),
+            shape((GROUP - 1, half // GROUP, width), f32),
             shape((width, 2 * padded), f32),
             shape((3, 3, 8, width), f32),
             shape((3, 8, 2 * padded), f32),
         ],
         in_specs=[HBM] * 5,
-        out_specs=[HBM] * 5,
+        out_specs=[HBM] * 6,
         scratch_shapes=[
             vmem((count, width), bf16),
             vmem((count, width), bf16),
@@ -1116,13 +1175,13 @@
             vmem((rounds, 8, width), f32),
             vmem((3, 3, 8, width), f32),
             vmem((3, 8, 2 * padded), f32),
-            dma((3 + 4 * chunks + 5,)),
+            dma((3 + 4 * chunks + GROUP + 5,)),
             dma((chunks + rounds,)),
             dma((chunks,)),
             dma((rounds,)),
         ],
         compiler_params=pltpu.CompilerParams(
-            collective_id=1, has_side_effects=True, vmem_limit_bytes=48 << 20
+            collective_id=1, has_side_effects=True, vmem_limit_bytes=60 << 20
         ),
         cost_estimate=pl.CostEstimate(flops=10**10, bytes_accessed=2 * 10**7, transcendentals=0),
         name="units",
@@ -1205,7 +1264,7 @@
             dma((1,)),
         ],
         compiler_params=pltpu.CompilerParams(
-            collective_id=2, has_side_effects=True, vmem_limit_bytes=40 << 20
+            collective_id=2, has_side_effects=True, vmem_limit_bytes=60 << 20
         ),
         cost_estimate=pl.CostEstimate(flops=10**10, bytes_accessed=2 * 10**7, transcendentals=0),
         name="grads",
@@ -1245,7 +1304,9 @@
 
 def turn_kernel(
     lines,
-    second_cot,
+    come,
+    back_own,
+    factors,
     residual,
     gains,
     cots,
@@ -1257,6 +1318,8 @@
     sums_out,
     out_factors,
     second_v,
+    own_v,
+    factors_v,
     residual_v,
     gains_v,
     cots_v,
@@ -1278,7 +1341,9 @@
     depth = attended.shape[1]
     bf16 = attended_v.dtype
     pairs = (
-        (second_cot, second_v),
+        (come, second_v),
+        (back_own, own_v),
+        (factors, factors_v),
         (residual, residual_v),
         (gains, gains_v),
         (cots, cots_v),
@@ -1288,7 +1353,7 @@
     loads = [moves.start(source, target) for source, target in pairs]
     meet_twin(seat)
     wires = Wires(send_sem)
-    for load in loads[:4]:
+    for load in loads[:6]:
         load.wait()
     sums_v[...] = jnp.zeros_like(sums_v)
 
@@ -1296,7 +1361,7 @@
         start = pl.multiple_of(at * STEP, STEP)
         span = pl.ds(start, STEP)
         values, inverse = norm_rows(residual_v, start, STEP)
-        cot = second_v[span, :]
+        cot = own_v[span, :] + second_v[span, :] * factors_v[0, 1, 0:1, :]
         sums_v[...] += folded(cot * values * inverse)
         total = cots_v[span, :].astype(jnp.float32) + norm_back(
             values, inverse, gains_v[8:9, :], cot
@@ -1309,7 +1374,7 @@
     wires.send(half_of(seq_v, core), half_of(seq_v, core), come_sem.at[0], seat.twin())
     moves.put(residual_v, residual_cot)
     moves.put(sums_v, sums_out)
-    for load in loads[4:]:
+    for load in loads[6:]:
         load.wait()
     wires.arrived(half_of(seq_v, 1 - core), come_sem.at[0], seat.twin())
 
@@ -1329,13 +1394,13 @@
     wires.drain()
 
 
-def turn(second_cot, residual, gains, cots, attended, out_full):
+def turn(come, back_own, factors, residual, gains, cots, attended, out_full):
     lines = lax.axis_size("dp") // GROUP
     half, width = residual.shape
     depth = attended.shape[1]
     f32, bf16 = jnp.float32, attended.dtype
     shape, vmem, dma = jax.ShapeDtypeStruct, pltpu.VMEM, pltpu.SemaphoreType.DMA
-    sources = (second_cot, residual, gains, cots, attended, out_full)
+    sources = (come, back_own, factors, residual, gains, cots, attended, out_full)
     return pl.pallas_call(
         functools.partial(turn_kernel, lines),
         out_shape=[
@@ -1589,7 +1654,7 @@
     )(pieces)
 
 
-def grouped_shards(
+def grouped_layer(
     block_input,
     attn_gain,
     query_weight,
@@ -1619,11 +1684,6 @@
     gains = jnp.stack([attn_gain, ffn_gain])
     gains = jnp.pad(gains, ((0, 6), (0, whole_up(rows, LANES) - rows)))
 
-    def shares(weight):
-        parts = weight.reshape(rows, lines, GROUP, unit_rows).transpose(2, 0, 1, 3)
-        return jnp.pad(parts.reshape(GROUP, rows, share), ((0, 0), (0, 0), (0, padded - share)))
-
-    pieces = jnp.concatenate([shares(gate_weight), shares(up_weight)], axis=2)
     length = 2 * block_input.shape[0]
     cosine, sine = rope_tables(length, HD)
     still, none = jnp.ones((length, HD), f32), jnp.zeros((length, HD), f32)
@@ -1650,7 +1710,16 @@
         attn_rows,
         residual,
     ) = front(
-        gains, narrow, output_weight, pieces, down_weight, block_input, output_cotangent, tables
+        gains,
+        narrow,
+        output_weight,
+        gate_weight,
+        up_weight,
+        down_weight,
+        block_input,
+        output_cotangent,
+        tables,
+        padded,
     )
     cot_rows = cot_rows.reshape(-1, width)
     ffn_rows = ffn_rows.reshape(-1, width)
@@ -1658,31 +1727,38 @@
     down_share = downs.reshape(share, width)
     half = block_input.shape[0]
 
-    hidden, back_sum, wide_grad, factors, wide_factors = units(
+    hidden, back_own, back_away, wide_grad, factors, wide_factors = units(
         ffn_rows, cot_rows, wide_full, down_share, gains_rows, padded
     )
-    back_sum = back_sum.reshape(GROUP, half, width)
-    back_out = [narrowed(back_sum[key], factors[0, 0, :1]) for key in range(1, GROUP)]
+    back_out = [back_away[key].astype(jnp.float16) for key in range(GROUP - 1)]
     back_in = exchanged(back_out, partner)
 
     wide_grad = after(wide_grad.reshape(lines, GROUP * rows, 2 * padded), *back_out)
-    wide_out = messages_of(wide_grad, wide_factors[0, :1], own)
-    wide_in = exchanged(wide_out, across)
-    hidden = after(hidden, *wide_out)
+    wide_undo = wide_factors[1, :1]
+    wide_out, wide_near, wide_second, wide_ended = line_halves(
+        wide_grad, wide_factors[0, :1], wide_undo
+    )
+    hidden = after(hidden, wide_out)
     down_grad, forth_sum = grads(cot_rows, hidden, down_share)
-    down_grad = down_grad.reshape(lines, unit_rows, width)
-    down_out = messages_of(down_grad, factors[1, 0, :1], own)
-    down_in = exchanged(down_out, across)
-
-    back_in = after(back_in, *down_out)
-    second_cot = added(back_sum[0], back_in, factors[0, 1, :1])
+    down_out, down_near, down_second, down_ended = line_halves(
+        down_grad.reshape(lines, unit_rows, width), factors[1, 0, :1], factors[1, 1, :1]
+    )
+
+    back_in = after(back_in, down_out)
+    come = sum(message.astype(f32) for message in back_in)
+    forth_sum = after(forth_sum.reshape(GROUP, half, width), come)
+    forth_out = [narrowed(forth_sum[key], factors[2, 0, :1]) for key in range(1, GROUP)]
+    forth_in = exchanged(forth_out, partner)
+    back_own = after(back_own, *forth_out)
     residual_cot, mix, out_grad, sums, out_factors = turn(
-        second_cot, residual, gains_rows, output_cotangent, attn_rows, out_full
+        come, back_own, factors, residual, gains_rows, output_cotangent, attn_rows, out_full
     )
     out_grad = out_grad.reshape(lines, GROUP, -1, width)
     out_out = group_messages(out_grad, place, out_factors[0, :1], out_factors[2])
     out_in = exchanged(out_out, partner)
-    residual_cot = after(residual_cot, *out_out)
+    wide_near = after(wide_near, *out_out)
+    wide_next, wide_far = wide_second(wide_near)
+    residual_cot = after(residual_cot, wide_next)
     input_grad, narrow_grad, narrow_factors = rear(
         residual_cot,
         mix,
@@ -1699,37 +1775,33 @@
     narrow_out = group_messages(narrow_grad, place, narrow_factors[0, :1], narrow_factors[2])
     narrow_in = exchanged(narrow_out, partner)
 
-    forth_sum = after(forth_sum.reshape(GROUP, half, width), *narrow_out)
-    forth_out = [narrowed(forth_sum[key], factors[2, 0, :1]) for key in range(1, GROUP)]
-    forth_in = exchanged(forth_out, partner)
-    out_in = after(out_in, *forth_out)
+    down_near = after(down_near, *narrow_out)
+    down_next, down_far = down_second(down_near)
+    out_in = after(out_in, down_next)
     out_undos = [undo_of(message) for message in out_in]
     out_sum = lax.dynamic_index_in_dim(out_grad, place, 1, keepdims=False)
     out_sum = added_noted(out_sum, out_in, out_undos)
     out_line = line_messages(out_sum, raised(out_factors[1, :1], out_undos), own)
     out_line_in = exchanged(out_line, across)
-    wide_in = after(wide_in, *out_line)
-    wide_undo = wide_factors[1, :1]
-    wide_own = added(lax.dynamic_index_in_dim(wide_grad, own, 0, keepdims=False), wide_in, wide_undo)
-    wide_own = wide_own.reshape(GROUP, rows, 2 * padded)
+    wide_far = after(wide_far, *out_line)
+    wide_own = wide_ended(wide_near, wide_far).reshape(GROUP, rows, 2 * padded)
     share_out = messages_of(wide_own, 0.25 * wide_factors[0, :1], place)
-    share_in = exchanged(share_out, partner)
-    narrow_in = after(narrow_in, *share_out)
+    forth_in = after(forth_in, *share_out)
+    block_output = (residual + added(forth_sum[0], forth_in, factors[2, 1, :1])).astype(bf16)
+    narrow_in = after(narrow_in, block_output)
     narrow_undos = [undo_of(message) for message in narrow_in]
     narrow_sum = lax.dynamic_index_in_dim(narrow_grad, place, 1, keepdims=False)
     narrow_sum = added_noted(narrow_sum, narrow_in, narrow_undos)
     narrow_line = line_messages(narrow_sum, raised(narrow_factors[1, :1], narrow_undos), own)
     narrow_line_in = exchanged(narrow_line, across)
-    forth_in = after(forth_in, *narrow_line)
-    block_output = (residual + added(forth_sum[0], forth_in, factors[2, 1, :1])).astype(bf16)
-    share_in = after(share_in, block_output)
+    share_in = exchanged(after(share_out, *narrow_line), partner)
+    down_far = after(down_far, *narrow_line)
+    down_own = down_ended(down_near, down_far)
+    share_in = after(share_in, down_own)
     pieces = [lax.dynamic_index_in_dim(wide_own, place, 0, keepdims=False)]
     pieces += [message.astype(f32) * (4.0 * wide_undo) for message in share_in]
     gate_own, up_own = unshare(jnp.stack(pieces), share, lines)
-    down_in = after(down_in, gate_own, up_own)
-    down_own = lax.dynamic_index_in_dim(down_grad, own, 0, keepdims=False)
-    down_own = added(down_own, down_in, factors[1, 1, :1])
-    out_line_in = after(out_line_in, down_own)
+    out_line_in = after(out_line_in, gate_own, up_own)
     out_own = added_noted(
         lax.dynamic_index_in_dim(out_sum, own, 0, keepdims=False),
         out_line_in,
@@ -1754,6 +1826,10 @@
         up_own,
         down_own,
     )
+
+
+def grouped_shards(*arrays):
+    return grouped_layer(*arrays)
 
 
 def solution(mesh):
@@ -1771,7 +1847,7 @@
         P(("dp", "mp"), None),
     )
     members = mesh.shape["dp"]
-    fits = mesh.shape["mp"] == 2 and members in (2 * GROUP, 4 * GROUP)
+    fits = mesh.shape["mp"] == 2 and members == GROUP * GROUP
     return jax.shard_map(
         grouped_shards if fits else plain_shards,
         mesh=mesh,

time: 323 us -> 297 us (0.920)
  waiting for transfers between devices: 70.1 us -> 54.8 us
  local copies, waits for them, and re-layouts: 26.3 us -> 12.8 us
    unnamed x105 -> x47, local copies, waits for them, and re-layouts: 22.4 us -> 4.2 us
    ppermute x15, waiting for transfers between devices: 34 us -> 18.9 us  [partner(): return lax.ppermute(values, 'dp', pairs)]
    dynamic_slice x3 -> x5, local copies, waits for them, and re-layouts: 1.25 us -> 5.29 us  [the longest x2 3.41 us: line_halves(): away = lax.dynamic_index_in_dim(blocks, 1 - low, 1, keepdims=False)]
    mul x8 -> x4, other arithmetic: 3.86 us -> 0.01 us  [the longest x1 0.01 us: second(): message = narrowed(half(1 - high, near), 0.5 * scale)]
    ppermute x12 -> x10, starting transfers between devices: 13 us -> 15.9 us  [across(): return lax.ppermute(values, 'dp', pairs)]
    convert_element_type x5 -> x6, other arithmetic: 9.7 us -> 10.8 us  [narrowed(): return (values * scale).astype(jnp.float16)]
    ppermute x12 -> x10, waiting for transfers between devices: 36.1 us -> 35.9 us  [across(): return lax.ppermute(values, 'dp', pairs)]
  transfers between devices with their start and end apart: 27 -> 25, of which waited for: 11 -> 7; matrix products, arithmetic and copies ran while one was open for 11% -> 13% of each run, Pallas kernels for 11% -> 12%
where the time goes in v1:
time: 297 us; the launch traced here: 296 us
  Pallas kernels  155 us (52%)
  waiting for transfers between devices  54.8 us (18%)
  other arithmetic  38.8 us (13%)
  starting transfers between devices  32.9 us (11%)
  local copies, waits for them, and re-layouts  12.8 us (4%)
    pallas_call x1, Pallas kernels, front(): pl.pallas_call(functools.partial(front_kernel, lines), out_shape=results,...  92 us
    ppermute x10, waiting for transfers between devices, across(): return lax.ppermute(values, 'dp', pairs)  35.9 us
    pallas_call x1, Pallas kernels, units(): pl.pallas_call(functools.partial(units_kernel, lines, share), out_shape=[...  26.6 us
    ppermute x15, waiting for transfers between devices, partner(): return lax.ppermute(values, 'dp', pairs)  18.9 us
    ppermute x15, starting transfers between devices, partner(): return lax.ppermute(values, 'dp', pairs)  17.1 us
    pallas_call x1, Pallas kernels, rear(): pl.pallas_call(functools.partial(rear_kernel, lines, members), out_shape=...  15.9 us
    ppermute x10, starting transfers between devices, across(): return lax.ppermute(values, 'dp', pairs)  15.9 us
    convert_element_type x6, other arithmetic, narrowed(): return (values * scale).astype(jnp.float16)  10.8 us
  transfers between devices with their start and end apart: 25, of which 7 were waited for; matrix products, arithmetic and copies ran while one was open for 13% of the time, Pallas kernels for 12%

profile of v1, /device:TPU:10, one launch (start us, length us, event | category | flops | bytes accessed | tf_op | source)
XLA Modules:
  0.0 295.5 jit_solution(6267671529041368739)
XLA Ops:
  1.2 0.8 copy.28
  2.0 0.8 copy.29
  2.8 1.3 fusion.56.gains
  4.4 0.7 pad_maximum_fusion.14.narrow
  5.1 0.8 pad_maximum_fusion.7.tables
  6.0 92.0 %front.1 = (f32[16,1792]{1,0:T(8,128)}, bf16[1792,640]{1,0:T(8,128)(2,1)}, bf16[512,1792]{1,0:T(8,128)(2,1)}, bf16[4,4,112,768]{3,2,1,0:T(8,128)(2,1)}, bf16[4,8...) custom-call(bf16[8,128]{1,0:T(8,128)(2,1)} %fusion.56.gains, ...), custom_call_target="tpu_custom_call" | custom-call | tf_op jit(solution)/shard_map/front/pallas_call | solution.py:869
  97.9 26.6 %units.1 = (bf16[1024,384]{1,0:T(8,128)(2,1)}, f32[128,1792]{1,0:T(8,128)}, f32[3,128,1792]{2,1,0:T(8,128)}, f32[1792,768]{1,0:T(8,128)}, f32[3,3,8,1792]{3,2,1,0:T(8,128)}, /*index=5*/f32[3,8,768]{2,1,0:T(8,128)}) custom-call(bf16[1024,1792]{1,0:T(8,128)(2,1)} %bitcast.213, bf16[1024,1792]{1,0:T(8,128)(2,1)} %bitcast.211, bf16[1792,768]{1,0:T(8,128)(2,1)} %bitcast.214, ...), custom_call_target="tpu_custom_call" | custom-call | flops 10000000000 | bytes 20000000 | tf_op jit(solution)/shard_map/units/pallas_call | solution.py:1150
  124.5 1.9 convert.65
  126.5 1.1 slice_bitcast_fusion
  128.2 1.5 collective-permute-start.1
  129.7 1.4 collective-permute-start.2
  131.1 0.8 slice_reduce_fusion.6
  131.9 2.0 constant_dynamic-slice_fusion.10
  133.8 1.4 fusion
  135.2 2.1 collective-permute-start.6
  137.3 9.9 %grads.1 = (f32[352,1792]{1,0:T(8,128)}, f32[512,1792]{1,0:T(8,128)}) custom-call(bf16[1024,1792]{1,0:T(8,128)(2,1)} %bitcast.212, bf16[1024,384]{1,0:T(8,128)(2,1)} %get-tuple-element.88.hidden, bf16[352,1792]{1,0:T(8,128)(2,1)} %bitcast.216), custom_call_target="tpu_custom_call" | custom-call | flops 10000000000 | bytes 20000000 | tf_op jit(solution)/shard_map/grads/pallas_call | solution.py:1249
  147.2 1.4 constant_dynamic-slice_fusion.9
  148.7 0.9 fusion.6
  149.8 1.4 convert_add_fusion.come
  151.3 3.1 %fusion.17 = (f16[128,1792]{1,0:T(8,128)(2,1)}, f16[128,1792]{1,0:T(8,128)(2,1)}, f16[128,1792]{1,0:T(8,128)(2,1)}) fusion(f32[4,128,1792]{2,1,0:T(8,128)} %bitcast.200, f32[1792]{0:T(1024)S(1)} %get-tuple-element.178), kind=kLoop, calls=%fused_computation.34 | loop fusion | flops 1376256 | bytes 4135936 | tf_op jit(solution)/shard_map/convert_element_type | solution.py:289
  155.1 7.6 %turn.1 = (f32[128,1792]{1,0:T(8,128)S(1)}, bf16[256,512]{1,0:T(8,128)(2,1)S(1)}, f32[512,1792]{1,0:T(8,128)S(1)}, f32[8,1792]{1,0:T(8,128)S(1)}, f32[3,8,1792]{2,1,0:T(8,128)S(1)}) custom-call(f32[128,1792]{1,0:T(8,128)S(1)} %convert_add_fusion.come, f32[128,1792]{1,0:T(8,128)S(1)} %copy-done.11, f32[3,3,8,1792]{3,2,1,0:T(8,128)S(1)} %copy-done.4, ...), custom_call_target="tpu_custom_call" | custom-call | flops 10000000000 | bytes 20000000 | tf_op jit(solution)/shard_map/turn/pallas_call | solution.py:1404
  163.6 1.6 collective-permute-start.10
  165.1 1.5 collective-permute-start.8
  166.6 1.9 collective-permute-done.6
  169.2 2.6 fusion.3
  171.9 15.9 %rear.1 = (f32[128,1792]{1,0:T(8,128)S(1)}, f32[16,120,640]{2,1,0:T(8,128)S(1)}, f32[3,8,640]{2,1,0:T(8,128)S(1)}) custom-call(f32[128,1792]{1,0:T(8,128)S(1)} %get-tuple-element.104.residual_cot, bf16[256,512]{1,0:T(8,128)(2,1)S(1)} %get-tuple-element.105.mix, f32[8,1792]{1,0:T(8,128)S(1)} %get-tuple-element.106.sums, f32[16,1792]{1,0:T(8,128)S(1)} %copy-done.10, ...), custom_call_target="tpu_custom_call" | custom-call | flops 10000000000 | bytes 20000000 | tf_op jit(solution)/shard_map/rear/pallas_call | solution.py:1602
  187.8 1.6 constant_dynamic-slice_fusion
  189.8 1.5 pad_maximum_fusion.1
  191.3 1.4 collective-permute-start.4
  192.6 2.0 fusion.26
  194.6 1.4 collective-permute-start.5
  196.0 2.0 collective-permute-start.7
  198.1 0.7 collective-permute-start.12
  199.4 0.8 pad_maximum_fusion.11
  200.3 26.9 %collective-permute-done.7 = f16[448,768]{1,0:T(8,128)(2,1)} collective-permute-done((f16[448,768]{1,0:T(8,128)(2,1)}, f16[448,768]{1,0:T(8,128)(2,1)}, u32[]{:S(2)}, u32[]{:S(2)}) %collective-permute-start.7) | collective-permute-done | bytes 688160 | tf_op jit(solution)/shard_map/ppermute | solution.py:281
  227.7 1.9 fusion.5
  229.6 1.7 collective-permute-start.14
  231.4 0.8 fusion.27
  232.2 3.4 %collective-permute-start.24 = (f16[88,1792]{1,0:T(8,128)(2,1)}, f16[88,1792]{1,0:T(8,128)(2,1)}, u32[]{:S(2)}, u32[]{:S(2)}) collective-permute-start(f16[88,1792]{1,0:T(8,128)(2,1)} %fusion.26), channel_id=1, source_target_pairs={{0,16},{2,18},{4,20},{6,22},{8,24},{10,26},{12,28},{14,30},{16,0},... | collective-permute-start | bytes 946184 | tf_op jit(solution)/shard_map/ppermute | solution.py:281
  235.6 2.6 fusion.21
  238.2 2.6 collective-permute-start.19
  240.9 16.0 %collective-permute-done.13 = f16[488,640]{1,0:T(8,128)(2,1)} collective-permute-done((f16[488,640]{1,0:T(8,128)(2,1)}, f16[488,640]{1,0:T(8,128)(2,1)}, u32[]{:S(2)}, u32[]{:S(2)}) %collective-permute-start.13) | collective-permute-done | bytes 624672 | tf_op jit(solution)/shard_map/ppermute | solution.py:276
  256.9 0.7 convert_reduce_fusion.10
  257.6 0.7 convert_reduce_fusion.11
  258.4 2.2 fusion.8
  260.7 0.8 pad_maximum_fusion.8
  261.7 0.7 collective-permute-start.21
  262.5 1.4 collective-permute-start.22
  263.8 1.4 collective-permute-start.23
  265.2 2.2 fusion.23
  267.4 1.5 collective-permute-done.21
  269.0 1.2 collective-permute-start.20
  270.1 1.3 collective-permute-done.22
  271.5 3.1 %collective-permute-start.15 = (f16[128,640]{1,0:T(8,128)(2,1)}, f16[128,640]{1,0:T(8,128)(2,1)S(1)}, u32[]{:S(2)}, u32[]{:S(2)}) collective-permute-start(f16[128,640]{1,0:T(8,128)(2,1)} %get-tuple-element.225), channel_id=1, source_target_pairs={{0,8},{2,10},{4,12},{6,14},{8,0},{10,2},{12,4},{14,6},{16,24},{18,... | collective-permute-start | bytes 491528 | tf_op jit(solution)/shard_map/ppermute | solution.py:281
  275.0 1.2 pad_maximum_fusion.pieces
  276.2 2.9 unshare.1
  279.1 1.2 collective-permute-start.17
  280.3 0.8 convert_reduce_fusion.1
  281.1 0.8 convert_reduce_fusion.2
  281.9 1.8 fusion.36
  283.7 2.2 collective-permute-done.16
  285.9 4.9 %collective-permute-done.17 = f16[128,640]{1,0:T(8,128)(2,1)S(1)} collective-permute-done((f16[128,640]{1,0:T(8,128)(2,1)S(1)}, f16[128,640]{1,0:T(8,128)(2,1)S(1)}, u32[]{:S(2)}, u32[]{:S(2)}) %collective-permute-start.17) | collective-permute-done | bytes 163872 | tf_op jit(solution)/shard_map/ppermute | solution.py:281
  290.8 1.1 fusion.34
  294.6 0.9 copy.33
  (111 shorter events, 8.7 us)
Async XLA Ops:
  0.6 3.7 %copy-start.20 = (bf16[112,512]{1,0:T(8,128)(2,1)S(1)}, bf16[112,512]{1,0:T(8,128)(2,1)}, u32[]{:S(2)}) copy-start(bf16[112,512]{1,0:T(8,128)(2,1)} %param.13) | copy-start | bytes 344068
  127.6 22.2 %collective-permute-start = (f16[128,1792]{1,0:T(8,128)(2,1)}, f16[128,1792]{1,0:T(8,128)(2,1)S(1)}, u32[]{:S(2)}, u32[]{:S(2)}) collective-permute-start(f16[128,1792]{1,0:T(8,128)(2,1)} %get-tuple-element.202), channel_id=1, source_target_pairs={{0,2},{2,0},{4,6},{6,4},{8,10},{10,8},{12,14},{14,12},{16,18},{18,... | collective-permute-start | bytes 1376264 | tf_op jit(solution)/shard_map/ppermute | solution.py:276
  128.2 21.6 %collective-permute-start.1 = (f16[128,1792]{1,0:T(8,128)(2,1)}, f16[128,1792]{1,0:T(8,128)(2,1)}, u32[]{:S(2)}, u32[]{:S(2)}) collective-permute-start(f16[128,1792]{1,0:T(8,128)(2,1)} %get-tuple-element.201), channel_id=1, source_target_pairs={{0,4},{2,6},{4,0},{6,2},{8,12},{10,14},{12,8},{14,10},{16,20},{18,... | collective-permute-start | bytes 1376264 | tf_op jit(solution)/shard_map/ppermute | solution.py:276
  129.7 20.1 %collective-permute-start.2 = (f16[128,1792]{1,0:T(8,128)(2,1)S(1)}, f16[128,1792]{1,0:T(8,128)(2,1)}, u32[]{:S(2)}, u32[]{:S(2)}) collective-permute-start(f16[128,1792]{1,0:T(8,128)(2,1)S(1)} %get-tuple-element.200), channel_id=1, source_target_pairs={{0,6},{2,4},{4,2},{6,0},{8,14},{10,12},{12,10},{14,8},{16,22},{18,... | collective-permute-start | bytes 1376264 | tf_op jit(solution)/shard_map/ppermute | solution.py:276
  135.2 33.3 %collective-permute-start.6 = (f16[896,768]{1,0:T(8,128)(2,1)}, f16[896,768]{1,0:T(8,128)(2,1)S(1)}, u32[]{:S(2)}, u32[]{:S(2)}) collective-permute-start(f16[896,768]{1,0:T(8,128)(2,1)} %fusion), channel_id=1, source_target_pairs={{0,8},{2,10},{4,12},{6,14},{8,0},{10,2},{12,4},{14,6},{16,24},{18,... | collective-permute-start | bytes 4128776 | tf_op jit(solution)/shard_map/ppermute | solution.py:281
  147.2 1.5 copy-start.4
  149.7 41.6 %collective-permute-start.11 = (f16[176,1792]{1,0:T(8,128)(2,1)}, f16[176,1792]{1,0:T(8,128)(2,1)}, u32[]{:S(2)}, u32[]{:S(2)}) collective-permute-start(f16[176,1792]{1,0:T(8,128)(2,1)} %fusion.6), channel_id=1, source_target_pairs={{0,8},{2,10},{4,12},{6,14},{8,0},{10,2},{12,4},{14,6},{16,24},{18,... | collective-permute-start | bytes 1892360 | tf_op jit(solution)/shard_map/ppermute | solution.py:281
  149.8 5.2 %copy-start.11 = (f32[128,1792]{1,0:T(8,128)S(1)}, f32[128,1792]{1,0:T(8,128)}, u32[]{:S(2)}) copy-start(f32[128,1792]{1,0:T(8,128)} %get-tuple-element.97.back_own) | copy-start | bytes 2752516
  151.3 3.7 %copy-start.1 = (f32[128,1792]{1,0:T(8,128)S(1)}, f32[128,1792]{1,0:T(8,128)}, u32[]{:S(2)}) copy-start(f32[128,1792]{1,0:T(8,128)} %get-tuple-element.77.residual) | copy-start | bytes 2752516
  151.3 3.7 %copy-start.2 = (bf16[128,1792]{1,0:T(8,128)(2,1)S(1)}, bf16[128,1792]{1,0:T(8,128)(2,1)}, u32[]{:S(2)}) copy-start(bf16[128,1792]{1,0:T(8,128)(2,1)} %cots.3) | copy-start | bytes 1376260
  151.3 3.7 %copy-start.6 = (bf16[512,1792]{1,0:T(8,128)(2,1)S(1)}, bf16[512,1792]{1,0:T(8,128)(2,1)}, u32[]{:S(2)}) copy-start(bf16[512,1792]{1,0:T(8,128)(2,1)} %get-tuple-element.99.out_full) | copy-start | bytes 5505028
  151.3 3.7 %copy-start.9 = (bf16[256,512]{1,0:T(8,128)(2,1)S(1)}, bf16[256,512]{1,0:T(8,128)(2,1)}, u32[]{:S(2)}) copy-start(bf16[256,512]{1,0:T(8,128)(2,1)} %get-tuple-element.98.attended) | copy-start | bytes 786436
  151.3 3.7 %copy-start.10 = (f32[16,1792]{1,0:T(8,128)S(1)}, f32[16,1792]{1,0:T(8,128)}, u32[]{:S(2)}) copy-start(f32[16,1792]{1,0:T(8,128)} %get-tuple-element.82.gains) | copy-start | bytes 344068
  154.4 75.2 %collective-permute-start.3 = (f16[128,1792]{1,0:T(8,128)(2,1)}, f16[128,1792]{1,0:T(8,128)(2,1)}, u32[]{:S(2)}, u32[]{:S(2)}) collective-permute-start(f16[128,1792]{1,0:T(8,128)(2,1)} %get-tuple-element.192), channel_id=1, source_target_pairs={{0,2},{2,0},{4,6},{6,4},{8,10},{10,8},{12,14},{14,12},{16,18},{18,... | collective-permute-start | bytes 1376264 | tf_op jit(solution)/shard_map/ppermute | solution.py:276
  163.2 8.6 %copy-start.5 = (bf16[1792,640]{1,0:T(8,128)(2,1)S(1)}, bf16[1792,640]{1,0:T(8,128)(2,1)}, u32[]{:S(2)}) copy-start(bf16[1792,640]{1,0:T(8,128)(2,1)} %get-tuple-element.108.narrow_full) | copy-start | bytes 6881284
  163.6 31.1 %collective-permute-start.10 = (f16[136,1792]{1,0:T(8,128)(2,1)S(1)}, f16[136,1792]{1,0:T(8,128)(2,1)S(1)}, u32[]{:S(2)}, u32[]{:S(2)}) collective-permute-start(f16[136,1792]{1,0:T(8,128)(2,1)S(1)} %get-tuple-element.220), channel_id=1, source_target_pairs={{0,6},{2,4},{4,2},{6,0},{8,14},{10,12},{12,10},{14,8},{16,22},{18,... | collective-permute-start | bytes 1462280 | tf_op jit(solution)/shard_map/ppermute | solution.py:276
  165.1 30.9 %collective-permute-start.8 = (f16[136,1792]{1,0:T(8,128)(2,1)S(1)}, f16[136,1792]{1,0:T(8,128)(2,1)S(1)}, u32[]{:S(2)}, u32[]{:S(2)}) collective-permute-start(f16[136,1792]{1,0:T(8,128)(2,1)S(1)} %get-tuple-element.222), channel_id=1, source_target_pairs={{0,2},{2,0},{4,6},{6,4},{8,10},{10,8},{12,14},{14,12},{16,18},{18,... | collective-permute-start | bytes 1462280 | tf_op jit(solution)/shard_map/ppermute | solution.py:276
  168.5 3.3 %copy-start.14 = (f16[896,768]{1,0:T(8,128)(2,1)}, f16[896,768]{1,0:T(8,128)(2,1)S(1)}, u32[]{:S(2)}) copy-start(f16[896,768]{1,0:T(8,128)(2,1)S(1)} %collective-permute-done.6) | copy-start | bytes 4128772
  168.5 29.6 %collective-permute-start.9 = (f16[136,1792]{1,0:T(8,128)(2,1)S(1)}, f16[136,1792]{1,0:T(8,128)(2,1)S(1)}, u32[]{:S(2)}, u32[]{:S(2)}) collective-permute-start(f16[136,1792]{1,0:T(8,128)(2,1)S(1)} %get-tuple-element.221), channel_id=1, source_target_pairs={{0,4},{2,6},{4,0},{6,2},{8,12},{10,14},{12,8},{14,10},{16,20},{18,... | collective-permute-start | bytes 1462280 | tf_op jit(solution)/shard_map/ppermute | solution.py:276
  169.2 2.6 copy-start
  169.2 2.6 copy-start.3
  169.2 2.6 copy-start.7
  169.2 2.7 copy-start.8
  191.3 40.9 %collective-permute-start.4 = (f16[128,1792]{1,0:T(8,128)(2,1)}, f16[128,1792]{1,0:T(8,128)(2,1)}, u32[]{:S(2)}, u32[]{:S(2)}) collective-permute-start(f16[128,1792]{1,0:T(8,128)(2,1)} %get-tuple-element.191), channel_id=1, source_target_pairs={{0,4},{2,6},{4,0},{6,2},{8,12},{10,14},{12,8},{14,10},{16,20},{18,... | collective-permute-start | bytes 1376264 | tf_op jit(solution)/shard_map/ppermute | solution.py:276
  194.6 41.0 %collective-permute-start.5 = (f16[128,1792]{1,0:T(8,128)(2,1)}, f16[128,1792]{1,0:T(8,128)(2,1)}, u32[]{:S(2)}, u32[]{:S(2)}) collective-permute-start(f16[128,1792]{1,0:T(8,128)(2,1)} %get-tuple-element.190), channel_id=1, source_target_pairs={{0,6},{2,4},{4,2},{6,0},{8,14},{10,12},{12,10},{14,8},{16,22},{18,... | collective-permute-start | bytes 1376264 | tf_op jit(solution)/shard_map/ppermute | solution.py:276
  196.0 31.1 %collective-permute-start.7 = (f16[448,768]{1,0:T(8,128)(2,1)}, f16[448,768]{1,0:T(8,128)(2,1)}, u32[]{:S(2)}, u32[]{:S(2)}) collective-permute-start(f16[448,768]{1,0:T(8,128)(2,1)} %fusion.3), channel_id=1, source_target_pairs={{0,16},{2,18},{4,20},{6,22},{8,24},{10,26},{12,28},{14,30},{16,0},... | collective-permute-start | bytes 2064392 | tf_op jit(solution)/shard_map/ppermute | solution.py:281
  198.1 40.1 %collective-permute-start.12 = (f16[488,640]{1,0:T(8,128)(2,1)}, f16[488,640]{1,0:T(8,128)(2,1)}, u32[]{:S(2)}, u32[]{:S(2)}) collective-permute-start(f16[488,640]{1,0:T(8,128)(2,1)} %get-tuple-element.228), channel_id=1, source_target_pairs={{0,2},{2,0},{4,6},{6,4},{8,10},{10,8},{12,14},{14,12},{16,18},{18,... | collective-permute-start | bytes 1873928 | tf_op jit(solution)/shard_map/ppermute | solution.py:276
  199.2 28.4 %copy-start.13 = (f32[128,1792]{1,0:T(8,128)}, f32[128,1792]{1,0:T(8,128)S(1)}, u32[]{:S(2)}) copy-start(f32[128,1792]{1,0:T(8,128)S(1)} %fusion.13) | copy-start | bytes 2752516
  199.4 28.3 %copy-start.15 = (f16[896,768]{1,0:T(8,128)(2,1)S(1)}, f16[896,768]{1,0:T(8,128)(2,1)}, u32[]{:S(2)}) copy-start(f16[896,768]{1,0:T(8,128)(2,1)} %copy-done.14) | copy-start | bytes 4128772
  227.2 29.7 %collective-permute-start.13 = (f16[488,640]{1,0:T(8,128)(2,1)}, f16[488,640]{1,0:T(8,128)(2,1)}, u32[]{:S(2)}, u32[]{:S(2)}) collective-permute-start(f16[488,640]{1,0:T(8,128)(2,1)} %get-tuple-element.227), channel_id=1, source_target_pairs={{0,4},{2,6},{4,0},{6,2},{8,12},{10,14},{12,8},{14,10},{16,20},{18,... | collective-permute-start | bytes 1873928 | tf_op jit(solution)/shard_map/ppermute | solution.py:276
  227.7 2.0 copy-start.16
  229.6 27.2 %collective-permute-start.14 = (f16[488,640]{1,0:T(8,128)(2,1)S(1)}, f16[488,640]{1,0:T(8,128)(2,1)S(1)}, u32[]{:S(2)}, u32[]{:S(2)}) collective-permute-start(f16[488,640]{1,0:T(8,128)(2,1)S(1)} %copy-done.16), channel_id=1, source_target_pairs={{0,6},{2,4},{4,2},{6,0},{8,14},{10,12},{12,10},{14,8},{16,22},{18,... | collective-permute-start | bytes 1873928 | tf_op jit(solution)/shard_map/ppermute | solution.py:276
  232.2 29.4 %collective-permute-start.24 = (f16[88,1792]{1,0:T(8,128)(2,1)}, f16[88,1792]{1,0:T(8,128)(2,1)}, u32[]{:S(2)}, u32[]{:S(2)}) collective-permute-start(f16[88,1792]{1,0:T(8,128)(2,1)} %fusion.26), channel_id=1, source_target_pairs={{0,16},{2,18},{4,20},{6,22},{8,24},{10,26},{12,28},{14,30},{16,0},... | collective-permute-start | bytes 946184 | tf_op jit(solution)/shard_map/ppermute | solution.py:281
  235.6 43.5 %collective-permute-start.18 = (f16[40,1792]{1,0:T(8,128)(2,1)}, f16[40,1792]{1,0:T(8,128)(2,1)}, u32[]{:S(2)}, u32[]{:S(2)}) collective-permute-start(f16[40,1792]{1,0:T(8,128)(2,1)} %get-tuple-element.219), channel_id=1, source_target_pairs={{0,8},{2,10},{4,12},{6,14},{8,0},{10,2},{12,4},{14,6},{16,24},{18,... | collective-permute-start | bytes 430088 | tf_op jit(solution)/shard_map/ppermute | solution.py:281
  238.2 42.1 %collective-permute-start.19 = (f16[40,1792]{1,0:T(8,128)(2,1)}, f16[40,1792]{1,0:T(8,128)(2,1)}, u32[]{:S(2)}, u32[]{:S(2)}) collective-permute-start(f16[40,1792]{1,0:T(8,128)(2,1)} %get-tuple-element.218), channel_id=1, source_target_pairs={{0,16},{2,18},{4,20},{6,22},{8,24},{10,26},{12,28},{14,30},{16,0},... | collective-permute-start | bytes 430088 | tf_op jit(solution)/shard_map/ppermute | solution.py:281
  256.9 1.5 copy-start.17
  260.6 6.8 %copy-start.12 = (f32[480,640]{1,0:T(8,128)}, f32[480,640]{1,0:T(8,128)S(1)}, u32[]{:S(2)}) copy-start(f32[480,640]{1,0:T(8,128)S(1)} %fusion.8) | copy-start | bytes 3686404
  260.6 1.1 copy-start.19
  260.6 1.8 copy-start.18
  261.7 7.2 %collective-permute-start.21 = (f16[112,768]{1,0:T(8,128)(2,1)S(1)}, f16[112,768]{1,0:T(8,128)(2,1)S(1)}, u32[]{:S(2)}, u32[]{:S(2)}) collective-permute-start(f16[112,768]{1,0:T(8,128)(2,1)S(1)} %copy-done.19), channel_id=1, source_target_pairs={{0,2},{2,0},{4,6},{6,4},{8,10},{10,8},{12,14},{14,12},{16,18},{18,... | collective-permute-start | bytes 516104 | tf_op jit(solution)/shard_map/ppermute | solution.py:276
  262.5 9.0 %collective-permute-start.22 = (f16[112,768]{1,0:T(8,128)(2,1)S(1)}, f16[112,768]{1,0:T(8,128)(2,1)S(1)}, u32[]{:S(2)}, u32[]{:S(2)}) collective-permute-start(f16[112,768]{1,0:T(8,128)(2,1)S(1)} %copy-done.18), channel_id=1, source_target_pairs={{0,4},{2,6},{4,0},{6,2},{8,12},{10,14},{12,8},{14,10},{16,20},{18,... | collective-permute-start | bytes 516104 | tf_op jit(solution)/shard_map/ppermute | solution.py:276
  263.8 10.8 %collective-permute-start.23 = (f16[112,768]{1,0:T(8,128)(2,1)S(1)}, f16[112,768]{1,0:T(8,128)(2,1)S(1)}, u32[]{:S(2)}, u32[]{:S(2)}) collective-permute-start(f16[112,768]{1,0:T(8,128)(2,1)S(1)} %get-tuple-element.130), channel_id=1, source_target_pairs={{0,6},{2,4},{4,2},{6,0},{8,14},{10,12},{12,10},{14,8},{16,22},{18,... | collective-permute-start | bytes 516104 | tf_op jit(solution)/shard_map/ppermute | solution.py:276
  269.0 11.3 %collective-permute-start.20 = (f16[40,1792]{1,0:T(8,128)(2,1)}, f16[40,1792]{1,0:T(8,128)(2,1)S(1)}, u32[]{:S(2)}, u32[]{:S(2)}) collective-permute-start(f16[40,1792]{1,0:T(8,128)(2,1)} %get-tuple-element.217), channel_id=1, source_target_pairs={{0,24},{2,26},{4,28},{6,30},{8,16},{10,18},{12,20},{14,22},{16,8},... | collective-permute-start | bytes 430088 | tf_op jit(solution)/shard_map/ppermute | solution.py:281
  271.5 12.2 %collective-permute-start.15 = (f16[128,640]{1,0:T(8,128)(2,1)}, f16[128,640]{1,0:T(8,128)(2,1)S(1)}, u32[]{:S(2)}, u32[]{:S(2)}) collective-permute-start(f16[128,640]{1,0:T(8,128)(2,1)} %get-tuple-element.225), channel_id=1, source_target_pairs={{0,8},{2,10},{4,12},{6,14},{8,0},{10,2},{12,4},{14,6},{16,24},{18,... | collective-permute-start | bytes 491528 | tf_op jit(solution)/shard_map/ppermute | solution.py:281
  274.6 11.3 %collective-permute-start.16 = (f16[128,640]{1,0:T(8,128)(2,1)}, f16[128,640]{1,0:T(8,128)(2,1)S(1)}, u32[]{:S(2)}, u32[]{:S(2)}) collective-permute-start(f16[128,640]{1,0:T(8,128)(2,1)} %get-tuple-element.224), channel_id=1, source_target_pairs={{0,16},{2,18},{4,20},{6,22},{8,24},{10,26},{12,28},{14,30},{16,0},... | collective-permute-start | bytes 491528 | tf_op jit(solution)/shard_map/ppermute | solution.py:281
  279.1 11.7 %collective-permute-start.17 = (f16[128,640]{1,0:T(8,128)(2,1)S(1)}, f16[128,640]{1,0:T(8,128)(2,1)S(1)}, u32[]{:S(2)}, u32[]{:S(2)}) collective-permute-start(f16[128,640]{1,0:T(8,128)(2,1)S(1)} %get-tuple-element.223), channel_id=1, source_target_pairs={{0,24},{2,26},{4,28},{6,30},{8,16},{10,18},{12,20},{14,22},{16,8},... | collective-permute-start | bytes 491528 | tf_op jit(solution)/shard_map/ppermute | solution.py:281
